TPU v7x, 8 devices: a whole 2x2x1 slice. The times are simulated.
8 devices in a mesh: emb: 2 (over z, y), col: 2 (over x), row: 2 (over core).
Axes of the slice: x: 2, y: 2, z: 1, core: 2. Of those that a mesh axis runs over, the one named last changes fastest.
Arguments:
- inter_mask: int32 [1024, 32768], P('row', 'col')
- emb_user: bfloat16 [1024, 64], P(('row', 'col'), 'emb')
- emb_item: bfloat16 [32768, 64], P(('col', 'row'), 'emb')
- triples: int32 [4096, 3], replicated
Outputs:
- output 1: bfloat16 [1024, 64], P(('row', 'col'), 'emb')
- output 2: bfloat16 [32768, 64], P(('col', 'row'), 'emb')
- output 3: float32 [4096], replicated
All inputs are finite; a program needn't handle non-finite values.
Results may differ from a plain program's by a relative error of at most 0.0178813.
Values are sent between devices in bfloat16 or wider.
A program may use at most 1 GiB of HBM per device.

v0:
```python
import jax
import jax.numpy as jnp
from jax import lax
from jax.sharding import PartitionSpec as P

NUM_LAYERS = 3


def lookup_rows(table, ids, offset):
    own_rows = table.shape[0]
    local_ids = ids - offset
    owned = (local_ids >= 0) & (local_ids < own_rows)
    picked = jnp.take(table, jnp.clip(local_ids, 0, own_rows - 1), axis=0)
    return jnp.where(owned[:, None], picked.astype(jnp.float32), 0.0)


def bpr_terms(final_user, final_item, triples, user_off, item_off):
    num_trip = triples.shape[0]
    fetched = jnp.concatenate([
        lookup_rows(final_user, triples[:, 0], user_off),
        lookup_rows(final_item, triples[:, 1], item_off),
        lookup_rows(final_item, triples[:, 2], item_off)], axis=0)
    fetched = lax.psum(fetched, ("row", "col"))
    e_user = fetched[:num_trip]
    e_pos = fetched[num_trip:2 * num_trip]
    e_neg = fetched[2 * num_trip:]
    score = lax.psum(jnp.sum(e_user * (e_pos - e_neg), axis=1), "emb")
    return jax.nn.softplus(-score)


def norm_adjacency(mask_blk):
    deg_user = lax.psum(jnp.sum(mask_blk, axis=1), "col")
    deg_item = lax.psum(jnp.sum(mask_blk, axis=0), "row")
    inv_user = lax.rsqrt(jnp.maximum(deg_user, 1).astype(jnp.float32))
    inv_item = lax.rsqrt(jnp.maximum(deg_item, 1).astype(jnp.float32))
    return ((inv_user[:, None] * mask_blk.astype(jnp.float32)) * inv_item[None, :]).astype(jnp.bfloat16)


def solution(mesh):
    n_col = mesh.shape["col"]
    n_row = mesh.shape["row"]

    def local_fn(mask_blk, user_sh, item_sh, triples):
        adj_blk = norm_adjacency(mask_blk)
        user_cur = user_sh
        item_cur = item_sh
        user_acc = user_sh.astype(jnp.float32)
        item_acc = item_sh.astype(jnp.float32)
        for layer_idx in range(NUM_LAYERS):
            item_panel = lax.all_gather(item_cur, "row", axis=0, tiled=True)
            user_part = jnp.dot(adj_blk, item_panel, preferred_element_type=jnp.float32)
            user_next = lax.psum_scatter(user_part, "col", scatter_dimension=0, tiled=True).astype(jnp.bfloat16)
            user_panel = lax.all_gather(user_cur, "col", axis=0, tiled=True)
            item_part = lax.dot_general(adj_blk, user_panel, (((0,), (0,)), ((), ())), preferred_element_type=jnp.float32)
            item_next = lax.psum_scatter(item_part, "row", scatter_dimension=0, tiled=True).astype(jnp.bfloat16)
            user_acc = user_acc + user_next.astype(jnp.float32)
            item_acc = item_acc + item_next.astype(jnp.float32)
            user_cur = user_next
            item_cur = item_next
        final_user = (user_acc / (NUM_LAYERS + 1)).astype(jnp.bfloat16)
        final_item = (item_acc / (NUM_LAYERS + 1)).astype(jnp.bfloat16)
        user_off = (lax.axis_index("row") * n_col + lax.axis_index("col")) * final_user.shape[0]
        item_off = (lax.axis_index("col") * n_row + lax.axis_index("row")) * final_item.shape[0]
        return final_user, final_item, bpr_terms(final_user, final_item, triples, user_off, item_off)

    return jax.shard_map(
        local_fn, mesh=mesh,
        in_specs=(P("row", "col"), P(("row", "col"), "emb"), P(("col", "row"), "emb"), P()),
        out_specs=(P(("row", "col"), "emb"), P(("col", "row"), "emb"), P()),
        check_vma=False)
```

profile of v0, /device:TPU:0, one launch (start us, length us, event | category | flops | bytes accessed | tf_op | source)
XLA Modules:
  0.0 261.5 jit_solution(14176503628034995375)
XLA Ops:
  7.2 13.1 %fusion.4 = (s32[512]{0:T(512)S(1)}, s32[16384]{0:T(1024)}) fusion(s32[512,16384]{1,0:T(8,128)} %param.6), kind=kLoop, calls=%fused_computation.33 | loop fusion | flops 16760320 | bytes 33622016 | tf_op jit(solution)/shard_map/reduce_sum | solution.py:32
  20.4 0.7 all-gather.4.cloned.1.call-update
  21.2 5.6 %psum.28 = s32[512]{0:T(512)S(1)} all-reduce(s32[512]{0:T(512)S(1)} %get-tuple-element.4), channel_id=1, replica_groups=mesh['emb'=2,'col'=2,'row'=2] {'col'}, use_global_device_ids=true, to_apply=%region_1.0 | all-reduce | flops 512 | bytes 4096 | tf_op jit(solution)/shard_map/psum | solution.py:32
  26.8 4.4 %all_gather.19 = bf16[512,32]{0,1:T(8,128)(2,1)S(1)} all-gather(bf16[256,32]{0,1:T(8,128)(2,1)S(1)} %copy-done.6), channel_id=1, replica_groups=mesh['emb'=2,'col'=2,'row'=2] {'col'}, dimensions={0}, use_global_device_ids=true | all-gather | bytes 49152 | tf_op jit(solution)/shard_map/all_gather | solution.py:53
  31.2 4.2 %all-reduce.3.cloned.1.call-done = s32[16384]{0:T(1024)} async-done(((s32[16384]{0:T(1024)}), s32[16384]{0:T(1024)}) %all-reduce.3.cloned.1.call-update) | async-done | bytes 65552 | tf_op jit(solution)/shard_map/psum | solution.py:33
  35.4 0.9 convert_rsqrt_fusion
  36.3 13.1 %multiply_convert_fusion = bf16[512,16384]{1,0:T(8,128)(2,1)S(1)} fusion(s32[512,16384]{1,0:T(8,128)} %param.6, f32[16384]{0:T(1024)S(1)} %convert_rsqrt_fusion, f32[512]{0:T(512)S(1)} %convert_rsqrt_fusion.1), kind=kLoop, calls=%fused_computation.3 | loop fusion | flops 33554432 | bytes 50399232 | tf_op jit(solution)/shard_map/convert_element_type | solution.py:36
  49.4 5.7 %copy-done = bf16[512,16384]{1,0:T(8,128)(2,1)} copy-done((bf16[512,16384]{1,0:T(8,128)(2,1)}, bf16[512,16384]{1,0:T(8,128)(2,1)S(1)}, u32[]{:S(2)}) %copy-start) | copy-done | bytes 16777240
  55.1 4.3 %fusion.8 = f32[16384,32]{0,1:T(8,128)} fusion(bf16[512,32]{0,1:T(8,128)(2,1)S(1)} %all_gather.19, bf16[512,16384]{1,0:T(8,128)(2,1)S(1)} %multiply_convert_fusion), kind=kOutput, calls=%fused_computation.37 | convolution fusion | flops 536870912 | bytes 18907136 | tf_op jit(solution)/shard_map/dot_general | solution.py:54
  59.5 0.0 reduce-scatter.7.cloned.1.call-start
  59.6 11.7 %fusion.5 = f32[512,32]{0,1:T(8,128)} fusion(bf16[512,16384]{1,0:T(8,128)(2,1)} %copy-done, bf16[16384,32]{0,1:T(8,128)(2,1)} %all-gather.4.cloned.1.call-done), kind=kOutput, calls=%fused_computation.34 | convolution fusion | flops 536870912 | bytes 17891328 | tf_op jit(solution)/shard_map/dot_general | solution.py:51
  71.3 0.0 all-gather.6.cloned.1.call-start
  71.4 2.1 convert_element_type.76
  73.5 0.0 reduce-scatter.11.cloned.1.call-start
  73.5 6.4 %reduce-scatter.7.cloned.1.call-done = f32[256,32]{0,1:T(8,128)} async-done(((f32[512,32]{0,1:T(8,128)}), f32[256,32]{0,1:T(8,128)}) %reduce-scatter.7.cloned.1.call-update) | async-done | bytes 32784 | tf_op jit(solution)/shard_map/reduce_scatter | solution.py:52
  79.9 0.8 convert_element_type.74
  80.7 4.6 %all_gather.21 = bf16[512,32]{0,1:T(8,128)(2,1)S(1)} all-gather(bf16[256,32]{0,1:T(8,128)(2,1)S(1)} %convert_element_type.74), channel_id=1, replica_groups=mesh['emb'=2,'col'=2,'row'=2] {'col'}, dimensions={0}, use_global_device_ids=true | all-gather | bytes 49152 | tf_op jit(solution)/shard_map/all_gather | solution.py:53
  85.3 2.7 %all-gather.6.cloned.1.call-done = bf16[16384,32]{0,1:T(8,128)(2,1)} async-done(((bf16[8192,32]{0,1:T(8,128)(2,1)}), bf16[16384,32]{0,1:T(8,128)(2,1)}) %all-gather.6.cloned.1.call-update) | async-done | bytes 1048592 | tf_op jit(solution)/shard_map/all_gather | solution.py:50
  88.0 11.7 %fusion.6 = f32[512,32]{0,1:T(8,128)} fusion(bf16[512,16384]{1,0:T(8,128)(2,1)} %copy-done, bf16[16384,32]{0,1:T(8,128)(2,1)} %all-gather.6.cloned.1.call-done), kind=kOutput, calls=%fused_computation.35 | convolution fusion | flops 536870912 | bytes 17891328 | tf_op jit(solution)/shard_map/dot_general | solution.py:51
  99.8 0.0 reduce-scatter.13.cloned.1.call-start
  99.9 10.2 %fusion.9 = f32[16384,32]{0,1:T(8,128)} fusion(bf16[512,32]{0,1:T(8,128)(2,1)S(1)} %all_gather.21, bf16[512,16384]{1,0:T(8,128)(2,1)} %copy-done), kind=kOutput, calls=%fused_computation.38 | convolution fusion | flops 536870912 | bytes 18907136 | tf_op jit(solution)/shard_map/dot_general | solution.py:54
  110.1 0.0 reduce-scatter.17.cloned.1.call-start
  110.2 0.8 convert_element_type.77
  110.9 4.4 %all_gather.23 = bf16[512,32]{0,1:T(8,128)(2,1)S(1)} all-gather(bf16[256,32]{0,1:T(8,128)(2,1)S(1)} %convert_element_type.77), channel_id=1, replica_groups=mesh['emb'=2,'col'=2,'row'=2] {'col'}, dimensions={0}, use_global_device_ids=true | all-gather | bytes 49152 | tf_op jit(solution)/shard_map/all_gather | solution.py:53
  115.3 10.1 %fusion.10 = f32[16384,32]{0,1:T(8,128)} fusion(bf16[512,32]{0,1:T(8,128)(2,1)S(1)} %all_gather.23, bf16[512,16384]{1,0:T(8,128)(2,1)} %copy-done), kind=kOutput, calls=%fused_computation.39 | convolution fusion | flops 536870912 | bytes 18907136 | tf_op jit(solution)/shard_map/dot_general | solution.py:54
  125.4 0.0 all-gather.8.cloned.1.call-start
  125.5 0.1 broadcast_clamp_fusion.2
  125.6 7.6 %reduce-scatter.17.cloned.1.call-done = f32[8192,32]{0,1:T(8,128)} async-done(((f32[16384,32]{0,1:T(8,128)}), f32[8192,32]{0,1:T(8,128)}) %reduce-scatter.17.cloned.1.call-update) | async-done | bytes 1048592 | tf_op jit(solution)/shard_map/reduce_scatter | solution.py:55
  133.2 2.7 %multiply_convert_fusion.1 = (bf16[8192,32]{0,1:T(8,128)(2,1)}, bf16[8192,32]{0,1:T(8,128)(2,1)}) fusion(bf16[8192,32]{0,1:T(8,128)(2,1)S(1)} %copy-done.2, f32[8192,32]{0,1:T(8,128)} %reduce-scatter.17.cloned.1.call-done, f32[8192,32]{0,1:T(8,128)} %reduce-scatter.13.cloned.1.call-done, f32[8192,32]{0,1:T(8,128)S(1)} %copy-done.1), kind=kLoop, calls=%fused_computation.8 | loop fusion | flops 3145728 | bytes 4718592 | tf_op jit(solution)/shard_map/convert_element_type | solution.py:61
  136.0 0.3 reduce-scatter.15.cloned.1.call-start
  136.3 0.3 and_reduce_fusion.2
  136.6 1.9 copy.11
  138.5 12.1 %gather_fusion.2 = bf16[4096,32]{1,0:T(8,128)(2,1)S(1)} fusion(bf16[8192,32]{1,0:T(8,128)(2,1)S(1)} %copy.11, s32[4096]{0:T(1024)S(1)} %fusion.3), kind=kCustom, calls=%fused_computation.1.clone | custom fusion | bytes 540672 | tf_op jit(solution)/shard_map/jit(_take)/gather | solution.py:13
  150.7 14.9 %gather_fusion.1 = bf16[4096,32]{1,0:T(8,128)(2,1)} fusion(bf16[8192,32]{1,0:T(8,128)(2,1)S(1)} %copy.11, s32[4096]{0:T(1024)S(1)} %fusion.2), kind=kCustom, calls=%fused_computation.clone | custom fusion | bytes 540672 | tf_op jit(solution)/shard_map/jit(_take)/gather | solution.py:13
  165.6 11.7 %fusion.7 = f32[512,32]{0,1:T(8,128)} fusion(bf16[512,16384]{1,0:T(8,128)(2,1)} %copy-done, bf16[16384,32]{0,1:T(8,128)(2,1)} %all-gather.8.cloned.1.call-done), kind=kOutput, calls=%fused_computation.36 | convolution fusion | flops 536870912 | bytes 17891328 | tf_op jit(solution)/shard_map/dot_general | solution.py:51
  177.4 7.0 %convert_select_fusion = (f32[4096,32]{1,0:T(8,128)}, f32[4096,32]{1,0:T(8,128)S(1)}) fusion(bf16[4096,32]{1,0:T(8,128)(2,1)S(1)} %gather_fusion.2, pred[4096]{0:T(1024)(128)(4,1)S(1)} %compare_and_fusion, pred[4096]{0:T(1024)(128)(4,1)S(1)} %get-tuple-element.14, bf16[4096,32]{1,0:T(8,128)(2,1)} %gather_fusion.1, pred[4096]{0:T(1024)(128)(4,1)S(1)} %compare_and_fusion.1, ...), kind=kLoop, calls=%fused_computation.4 | loop fusion | flops 786432 | bytes 1589248 | tf_op jit(solution)/shard_map/jit(_where)/select_n | solution.py:14
  184.4 3.0 %copy.15 = f32[4096,32]{0,1:T(8,128)} copy(f32[4096,32]{1,0:T(8,128)} %get-tuple-element.18) | data formatting | bytes 1048576 | tf_op jit(solution)/shard_map/jit(_where)/select_n | solution.py:14
  187.4 1.4 copy.14
  188.8 0.8 multiply_convert_fusion.2
  189.6 0.1 copy.10
  189.7 12.1 %gather_fusion = bf16[4096,32]{1,0:T(8,128)(2,1)S(1)} fusion(bf16[256,32]{1,0:T(8,128)(2,1)S(1)} %copy.10, s32[4096]{0:T(1024)S(1)} %broadcast_clamp_fusion), kind=kCustom, calls=%fused_computation.2 | custom fusion | bytes 540672 | tf_op jit(solution)/shard_map/jit(_take)/gather | solution.py:13
  201.8 1.3 convert_select_fusion.2
  203.1 0.6 copy.13
  203.7 2.5 pad_maximum_fusion
  206.2 38.6 %all-reduce.5.cloned.1.call-done = f32[12288,32]{0,1:T(8,128)} async-done(((f32[12288,32]{0,1:T(8,128)}), f32[12288,32]{0,1:T(8,128)}) %all-reduce.5.cloned.1.call-update) | async-done | bytes 1572880 | tf_op jit(solution)/shard_map/psum | solution.py:23
  244.7 1.4 fusion.1
  246.2 8.1 %psum.31 = f32[4096]{0:T(1024)S(1)} all-reduce(f32[4096]{0:T(1024)S(1)} %fusion.1), channel_id=1, replica_groups=mesh['emb'=2,'col'=2,'row'=2] {'emb'}, use_global_device_ids=true, to_apply=%region_12.14 | all-reduce | flops 4096 | bytes 32768 | tf_op jit(solution)/shard_map/psum | solution.py:27
  254.3 0.6 compare_select_fusion.3
  (41 shorter events, 0.5 us)
Async XLA Ops:
  7.2 19.6 %copy-start.6 = (bf16[256,32]{0,1:T(8,128)(2,1)S(1)}, bf16[256,32]{0,1:T(8,128)(2,1)}, u32[]{:S(2)}) copy-start(bf16[256,32]{0,1:T(8,128)(2,1)} %param.7) | copy-start | bytes 49156
  7.2 28.2 %all-reduce.3.cloned.1.call-start = ((), (), s32[]{:S(2)}) async-start(), calls=%async_computation.6 | async-start | bytes 131072 | tf_op jit(solution)/shard_map/psum | solution.py:33
  20.4 39.2 %all-gather.4.cloned.1.call-start = ((), (), s32[]{:S(2)}) async-start(), calls=%async_computation.7 | async-start | bytes 1572864 | tf_op jit(solution)/shard_map/all_gather | solution.py:50
  21.1 50.3 %reduce-scatter.9.cloned.1.call-start = ((), (), s32[]{:S(2)}) async-start(), calls=%async_computation.9 | async-start | bytes 3145728 | tf_op jit(solution)/shard_map/reduce_scatter | solution.py:55
  49.4 5.7 %copy-start = (bf16[512,16384]{1,0:T(8,128)(2,1)}, bf16[512,16384]{1,0:T(8,128)(2,1)S(1)}, u32[]{:S(2)}) copy-start(bf16[512,16384]{1,0:T(8,128)(2,1)S(1)} %multiply_convert_fusion) | copy-start | bytes 50331652
  59.5 20.4 %reduce-scatter.7.cloned.1.call-start = ((), (), s32[]{:S(2)}) async-start(), calls=%async_computation.8 | async-start | bytes 98304 | tf_op jit(solution)/shard_map/reduce_scatter | solution.py:52
  71.3 16.7 %all-gather.6.cloned.1.call-start = ((), (), s32[]{:S(2)}) async-start(), calls=%async_computation.10 | async-start | bytes 1572864 | tf_op jit(solution)/shard_map/all_gather | solution.py:50
  73.5 36.7 %reduce-scatter.11.cloned.1.call-start = ((), (), s32[]{:S(2)}) async-start(), calls=%async_computation.11 | async-start | bytes 98304 | tf_op jit(solution)/shard_map/reduce_scatter | solution.py:52
  99.8 25.7 %copy-start.5 = (s32[4096,3]{0,1:T(4,128)S(1)}, s32[4096,3]{0,1:T(4,128)}, u32[]{:S(2)}) copy-start(s32[4096,3]{0,1:T(4,128)} %param.9) | copy-start | bytes 147460
  99.8 33.5 %copy-start.1 = (f32[8192,32]{0,1:T(8,128)S(1)}, f32[8192,32]{0,1:T(8,128)}, u32[]{:S(2)}) copy-start(f32[8192,32]{0,1:T(8,128)} %reduce-scatter.9.cloned.1.call-done) | copy-start | bytes 3145732
  99.8 33.5 %copy-start.2 = (bf16[8192,32]{0,1:T(8,128)(2,1)S(1)}, bf16[8192,32]{0,1:T(8,128)(2,1)}, u32[]{:S(2)}) copy-start(bf16[8192,32]{0,1:T(8,128)(2,1)} %param.8) | copy-start | bytes 1572868
  99.8 25.8 %reduce-scatter.13.cloned.1.call-start = ((), (), s32[]{:S(2)}) async-start(), calls=%async_computation.12 | async-start | bytes 3145728 | tf_op jit(solution)/shard_map/reduce_scatter | solution.py:55
  110.1 23.1 %reduce-scatter.17.cloned.1.call-start = ((), (), s32[]{:S(2)}) async-start(), calls=%async_computation.15 | async-start | bytes 3145728 | tf_op jit(solution)/shard_map/reduce_scatter | solution.py:55
  125.4 40.2 %all-gather.8.cloned.1.call-start = ((), (), s32[]{:S(2)}) async-start(), calls=%async_computation.13 | async-start | bytes 1572864 | tf_op jit(solution)/shard_map/all_gather | solution.py:50
  136.0 52.8 %reduce-scatter.15.cloned.1.call-start = ((), (), s32[]{:S(2)}) async-start(), calls=%async_computation.14 | async-start | bytes 98304 | tf_op jit(solution)/shard_map/reduce_scatter | solution.py:52
  165.6 23.2 %copy-start.3 = (f32[256,32]{0,1:T(8,128)S(1)}, f32[256,32]{0,1:T(8,128)}, u32[]{:S(2)}) copy-start(f32[256,32]{0,1:T(8,128)} %reduce-scatter.7.cloned.1.call-done) | copy-start | bytes 98308
  165.6 23.2 %copy-start.4 = (f32[256,32]{0,1:T(8,128)S(1)}, f32[256,32]{0,1:T(8,128)}, u32[]{:S(2)}) copy-start(f32[256,32]{0,1:T(8,128)} %reduce-scatter.11.cloned.1.call-done) | copy-start | bytes 98308
  177.4 67.3 %all-reduce.5.cloned.1.call-start = ((), (), s32[]{:S(2)}) async-start(), calls=%async_computation.16 | async-start | bytes 3145728 | tf_op jit(solution)/shard_map/psum | solution.py:23
  189.6 65.4 %copy-start.7 = (bf16[256,32]{0,1:T(8,128)(2,1)}, bf16[256,32]{0,1:T(8,128)(2,1)S(1)}, u32[]{:S(2)}) copy-start(bf16[256,32]{0,1:T(8,128)(2,1)S(1)} %multiply_convert_fusion.2) | copy-start | bytes 49156
Sparse Core Ops, SparseCore 0:
  20.5 14.8 all-reduce.2
  36.9 7.3 all-gather.3
  59.6 7.7 reduce-scatter.8
  71.4 8.4 reduce-scatter.6
  81.9 6.1 all-gather.5
  99.9 8.4 reduce-scatter.10
  110.6 7.3 reduce-scatter.12
  125.5 7.6 reduce-scatter.16
  136.1 7.2 all-gather.7
  177.5 8.3 reduce-scatter.14
  206.3 38.3 all-reduce.4
where the time goes:
time: 262 us; the launch traced here: 261 us
  waiting for transfers between devices  60.5 us (23%)
  matrix products  59.8 us (23%)
  local copies, waits for them, and re-layouts  51.9 us (20%)
  other arithmetic  47.4 us (18%)
  blocking collectives  27.1 us (10%)
  between operations  14.1 us (5%)
    gather x3, local copies, waits for them, and re-layouts, lookup_rows(): picked = jnp.take(table, jnp.clip(local_ids, 0, own_rows - 1), axis=0)  39.2 us
    psum x1, waiting for transfers between devices, bpr_terms(): fetched = lax.psum(fetched, ('row', 'col'))  38.6 us
    dot_general x3, matrix products, local_fn(): user_part = jnp.dot(adj_blk, item_panel, preferred_element_type=jnp.float32)  35.2 us
    dot_general x3, matrix products, local_fn(): lax.dot_general(adj_blk, user_panel, (((0,), (0,)), ((), ())), preferred_...  24.6 us
    all_gather x3, blocking collectives, local_fn(): user_panel = lax.all_gather(user_cur, 'col', axis=0, tiled=True)  13.4 us
    convert_element_type x1, other arithmetic, norm_adjacency(): (inv_user[:, None] * mask_blk.astype(jnp.float32) * inv_item[None, :]).as...  13.1 us
    reduce_sum x1, other arithmetic, norm_adjacency(): deg_user = lax.psum(jnp.sum(mask_blk, axis=1), 'col')  13.1 us
    select_n x2, other arithmetic, lookup_rows(): return jnp.where(owned[:, None], picked.astype(jnp.float32), 0.0)  8.24 us
  transfers between devices with their start and end apart: 11, of which 5 were waited for; matrix products, arithmetic and copies ran while one was open for 36% of the time, Pallas kernels for 0%

commit v1 on v0

v1 whole, which is shorter than its diff:
```python
import functools

import jax
import jax.numpy as jnp
from jax import lax
from jax.experimental import pallas as pl
from jax.experimental.pallas import tpu as pltpu
from jax.sharding import PartitionSpec as P

NUM_LAYERS = 3
CH = 1024
NSLOT = 5
MESH = pl.DeviceIdType.MESH
F32 = jnp.float32
BF16 = jnp.bfloat16


def remote(src, dst, ssem, rsem, dev):
    return pltpu.make_async_remote_copy(src_ref=src, dst_ref=dst, send_sem=ssem, recv_sem=rsem,
                                        device_id=dev, device_id_type=MESH)


def kernel(n_usr, n_itm, dim, n_trip,
           mask_ref, eu_ref, ei_ref, tri_ref, ou_ref, oi_ref, loss_ref,
           stage, adj, rowacc, degi, degi_r, degu, degu_r, invu, invi,
           it0, it1, it2, ut0, i1p, i1r, i2p, i2r, i3p, i3r,
           up, up_r, u3p, u3_r, ufin, ufin_r, ofin, oufin, table, utab,
           tri_v, idx_v, idx_s, dbuf, drecv, sbuf, srecv, lbuf,
           msem, lsem, ssem, rsem, cs1, cr1, cs2, cr2, cs3, cr3, ds, dr, bs, br):
    e = lax.axis_index("emb")
    c = lax.axis_index("col")
    r = lax.axis_index("row")
    sib = {"row": 1 - r}
    xpeer = {"col": 1 - c}
    nch = n_itm // CH
    half = n_itm // 2
    hch = nch // 2
    uh = n_usr // 2
    nhome = n_trip // 4
    hrow = nhome // 4

    def mask_copy(j):
        slot = lax.rem(j, NSLOT)
        return pltpu.make_async_copy(mask_ref.at[:, pl.ds(j * CH, CH)], stage.at[slot], msem.at[slot])

    for j in range(NSLOT):
        mask_copy(j).start()
    own_i = it0.at[:, pl.ds(pl.multiple_of(r * half, half), half)]
    own_u = ut0.at[:, pl.ds(pl.multiple_of(c * uh, uh), uh)]
    cp_i = pltpu.make_async_copy(ei_ref, own_i, lsem.at[0])
    cp_u = pltpu.make_async_copy(eu_ref, own_u, lsem.at[1])
    cp_t = pltpu.make_async_copy(tri_ref, tri_v, lsem.at[2])
    cp_i.start()
    cp_u.start()
    cp_t.start()

    barrier = pltpu.get_barrier_semaphore()
    for q in range(1, 8):
        dev = {"emb": lax.rem(e + q // 4, 2), "col": lax.rem(c + (q // 2) % 2, 2), "row": lax.rem(r + q % 2, 2)}
        pl.semaphore_signal(barrier, inc=1, device_id=dev, device_id_type=MESH)

    rowacc[...] = jnp.zeros_like(rowacc)

    def mask_step(j, _):
        slot = lax.rem(j, NSLOT)
        mask_copy(j).wait()
        cols = pl.ds(pl.multiple_of(j * CH, CH), CH)

        def rows_step(g, acc):
            rows = pl.ds(pl.multiple_of(g * 16, 16), 16)
            m = stage[slot, rows, :].astype(F32)
            adj[rows, cols] = m.astype(BF16)
            s = m[:, 0:128]
            for k in range(1, CH // 128):
                s = s + m[:, k * 128:(k + 1) * 128]
            rowacc[rows, :] += s
            return acc + (m[0:8] + m[8:16])

        acc = lax.fori_loop(0, n_usr // 16, rows_step, jnp.zeros((8, CH), F32), unroll=2)
        degi[pl.ds(j, 1), :] = jnp.sum(acc, axis=0, keepdims=True)

        @pl.when(j + NSLOT < nch)
        def _():
            mask_copy(j + NSLOT).start()
        return 0

    lax.fori_loop(0, 4, mask_step, 0)
    cp_i.wait()
    cp_u.wait()
    cp_t.wait()
    pl.semaphore_wait(barrier, 7)
    rc_i = remote(own_i, own_i, ssem.at[0], rsem.at[0], sib)
    rc_u = remote(own_u, own_u, ssem.at[1], rsem.at[1], xpeer)
    rc_i.start()
    rc_u.start()
    lax.fori_loop(4, nch, mask_step, 0)

    degu[...] = jnp.sum(rowacc[...].T, axis=0, keepdims=True)
    rc_du = remote(degu, degu_r, ssem.at[2], rsem.at[2], xpeer)
    rc_di = remote(degi, degi_r, ssem.at[3], rsem.at[3], sib)
    rc_du.start()
    rc_di.start()

    item_off = (c * 2 + r) * half
    for k in range(2):
        loc = tri_v[k + 1, :, :] - item_off
        idx_v[k, :, :] = jnp.where((loc >= 0) & (loc < half), loc, half)
    idx_v[2, :, :] = tri_v[0, :, :]
    cp_x = pltpu.make_async_copy(idx_v, idx_s, lsem.at[0])
    cp_x.start()
    table[pl.ds(half, 8), :] = jnp.zeros((8, 128), F32)

    rc_di.wait()
    invi[...] = lax.rsqrt(jnp.maximum(degi[...] + degi_r[...], 1.0))
    rc_i.wait()
    rc_u.wait()
    cp_x.wait()
    rc_du.wait()
    inv_row = lax.rsqrt(jnp.maximum(degu[...] + degu_r[...], 1.0))
    invu[...] = jnp.broadcast_to(inv_row, (128, n_usr)).T

    def chunk1(j):
        cols = pl.ds(pl.multiple_of(j * CH, CH), CH)
        return remote(i1p.at[:, cols], i1r.at[:, cols], cs1.at[j], cr1.at[j], sib)

    def build_step(j, _):
        cols = pl.ds(pl.multiple_of(j * CH, CH), CH)
        wi = jnp.broadcast_to(invi[pl.ds(j, 1), :], (16, CH))

        def rows_step(g, _):
            rows = pl.ds(pl.multiple_of(g * 16, 16), 16)
            wu = jnp.concatenate([invu[rows, :]] * (CH // 128), axis=1)
            adj[rows, cols] = (wu * wi).astype(BF16) * adj[rows, cols]
            return 0

        lax.fori_loop(0, n_usr // 16, rows_step, 0, unroll=4)
        i1p[:, cols] = jnp.dot(ut0[...], adj[:, cols], preferred_element_type=F32)
        chunk1(j).start()
        return 0

    lax.fori_loop(0, nch, build_step, 0)

    def dot_t(lhs, a):
        return lax.dot_general(lhs, a, (((1,), (1,)), ((), ())), preferred_element_type=F32)

    up[...] = jnp.zeros_like(up)

    def user_step(j, _):
        cols = pl.ds(pl.multiple_of(j * CH, CH), CH)
        chunk1(j).wait_recv()
        v1 = (i1p[:, cols] + i1r[:, cols]).astype(BF16)
        it1[:, cols] = v1
        lhs = jnp.concatenate([it0[:, cols], v1], axis=0)
        up[...] += dot_t(lhs, adj[:, cols])
        return 0

    lax.fori_loop(0, nch, user_step, 0)
    rc_up = remote(up, up_r, ssem.at[4], rsem.at[4], xpeer)
    rc_up.start()
    rc_up.wait()
    u12 = (up[...] + up_r[...]).astype(BF16)

    def chunk2(j):
        cols = pl.ds(pl.multiple_of(j * CH, CH), CH)
        return remote(i2p.at[:, cols], i2r.at[:, cols], cs2.at[j], cr2.at[j], sib)

    def chunk3(k, base):
        src = pl.ds(pl.multiple_of((base + k) * CH, CH), CH)
        dst = pl.ds(pl.multiple_of(k * CH, CH), CH)
        return remote(i3p.at[:, src], i3r.at[:, dst], cs3.at[k], cr3.at[k], sib)

    def item_step(k, base, send3):
        j = base + k
        cols = pl.ds(pl.multiple_of(j * CH, CH), CH)
        part = jnp.dot(u12, adj[:, cols], preferred_element_type=F32)
        i2p[:, cols] = part[0:dim]
        i3p[:, cols] = part[dim:2 * dim]
        chunk2(j).start()
        if send3:
            chunk3(k, base).start()
        return 0

    sbase = (1 - r) * hch
    obase = r * hch
    lax.fori_loop(0, hch, lambda k, _: item_step(k, sbase, True), 0)
    lax.fori_loop(0, hch, lambda k, _: item_step(k, obase, False), 0)

    u3p[...] = jnp.zeros_like(u3p)

    def user3_step(k, base):
        j = base + k
        cols = pl.ds(pl.multiple_of(j * CH, CH), CH)
        chunk2(j).wait_recv()
        v2 = (i2p[:, cols] + i2r[:, cols]).astype(BF16)
        it2[:, cols] = v2
        u3p[...] += dot_t(v2, adj[:, cols])
        return 0

    lax.fori_loop(0, hch, lambda k, _: user3_step(k, obase), 0)
    lax.fori_loop(0, hch, lambda k, _: user3_step(k, sbase), 0)
    rc_u3 = remote(u3p, u3_r, ssem.at[5], rsem.at[5], xpeer)
    rc_u3.start()

    def final_step(k, _):
        cols = pl.ds(pl.multiple_of((obase + k) * CH, CH), CH)
        loc = pl.ds(pl.multiple_of(k * CH, CH), CH)
        chunk3(k, sbase).wait_recv()
        v3 = (i3p[:, cols] + i3r[:, loc]).astype(BF16)
        acc = it0[:, cols].astype(F32) + it1[:, cols].astype(F32)
        acc = (acc + it2[:, cols].astype(F32)) + v3.astype(F32)
        fin = (acc * (1.0 / (NUM_LAYERS + 1))).astype(BF16)
        ofin[:, loc] = fin
        fin = fin.astype(F32)
        for b in range(CH // 128):
            blk = fin[:, b * 128:(b + 1) * 128]
            table[pl.ds(pl.multiple_of(k * CH + b * 128, 128), 128), :] = jnp.concatenate([blk] * 4, axis=0).T
        return 0

    lax.fori_loop(0, hch, final_step, 0)
    cp_oi = pltpu.make_async_copy(ofin, oi_ref, lsem.at[1])
    cp_oi.start()

    lane_blk = lax.broadcasted_iota(jnp.int32, (1, 128), 1) // dim

    def pack(rows4):
        d = rows4[0]
        for b in range(1, 4):
            d = jnp.where(lane_blk == b, rows4[b], d)
        return d

    def d_send(q, ah):
        hc, hr = lax.rem(c + q // 2, 2), lax.rem(r + q % 2, 2)
        rows = pl.ds(ah * 128, 128)
        return remote(dbuf.at[q, rows, :], drecv.at[q - 1, rows, :], ds.at[q - 1, ah], dr.at[q - 1, ah],
                      {"col": hc, "row": hr})

    def diff_rows(q, ah):
        home = lax.rem(c + q // 2, 2) * 2 + lax.rem(r + q % 2, 2)

        def body(al, _):
            out = []
            for b in range(4):
                row = home * (nhome // 128) + b * (hrow // 128) + ah
                p = idx_s[0, row, al]
                n = idx_s[1, row, al]
                out.append(table[pl.ds(p, 1), :] - table[pl.ds(n, 1), :])
            dbuf[q, pl.ds(ah * 128 + al, 1), :] = pack(out)
            return 0

        lax.fori_loop(0, 128, body, 0, unroll=8)

    for q in (3, 2, 1, 0):
        for ah in range(hrow // 128):
            diff_rows(q, ah)
            if q:
                d_send(q, ah).start()

    rc_u3.wait()
    u3 = (u3p[...] + u3_r[...]).astype(BF16).astype(F32)
    uacc = ut0[...].astype(F32) + u12[0:dim].astype(F32)
    uacc = (uacc + u12[dim:2 * dim].astype(F32)) + u3
    ufin[...] = (uacc * (1.0 / (NUM_LAYERS + 1))).astype(BF16)
    rc_uf = remote(ufin, ufin_r, ssem.at[6], rsem.at[6], sib)
    rc_uf.start()
    oufin[...] = ufin[:, pl.ds(pl.multiple_of(c * uh, uh), uh)]
    cp_ou = pltpu.make_async_copy(oufin, ou_ref, lsem.at[2])
    cp_ou.start()

    def user_table(src, base):
        for b in range(n_usr // 128):
            blk = src[:, b * 128:(b + 1) * 128].astype(F32)
            utab[pl.ds(pl.multiple_of(base + b * 128, 128), 128), :] = jnp.concatenate([blk] * 4, axis=0).T

    user_table(ufin, r * n_usr)
    rc_uf.wait()
    user_table(ufin_r, (1 - r) * n_usr)

    home = c * 2 + r
    for ah in range(hrow // 128):
        def ubody(al, _, ah=ah):
            out = []
            for b in range(4):
                row = home * (nhome // 128) + b * (hrow // 128) + ah
                out.append(utab[pl.ds(idx_s[2, row, al], 1), :])
            dbuf[4, pl.ds(ah * 128 + al, 1), :] = pack(out)
            return 0
        lax.fori_loop(0, 128, ubody, 0, unroll=8)

    for q in (3, 2, 1):
        for ah in range(hrow // 128):
            d_send(q, ah).wait()
    dsum = (dbuf[0] + drecv[0]) + (drecv[1] + drecv[2])
    prod = (dsum * dbuf[4]).T
    for b in range(4):
        s = jnp.sum(prod[b * dim:(b + 1) * dim, :], axis=0, keepdims=True)
        for h in range(hrow // 128):
            sbuf[pl.ds(b * (hrow // 128) + h, 1), :] = s[:, h * 128:(h + 1) * 128]

    def s_send(q):
        dev = {"emb": lax.rem(e + q // 4, 2), "col": lax.rem(c + (q // 2) % 2, 2), "row": lax.rem(r + q % 2, 2)}
        return remote(sbuf, srecv.at[q - 1], bs.at[q - 1], br.at[q - 1], dev)

    for q in range(7, 0, -1):
        s_send(q).start()
    for q in range(7, 0, -1):
        s_send(q).wait()
    for q in range(4):
        own = sbuf[...] if q == 0 else srecv[q - 1]
        x = own + srecv[q + 3]
        hq = lax.rem(c + q // 2, 2) * 2 + lax.rem(r + q % 2, 2)
        ls = jnp.maximum(-x, 0.0) + jnp.log1p(jnp.exp(-jnp.abs(x)))
        lbuf[pl.ds(pl.multiple_of(hq * (nhome // 128), 8), nhome // 128), :] = ls
    cp_l = pltpu.make_async_copy(lbuf, loss_ref, lsem.at[0])
    cp_l.start()

    def drain(j, _):
        chunk1(j).wait_send()
        chunk2(j).wait_send()
        return 0
    lax.fori_loop(0, nch, drain, 0)

    def drain3(k, _):
        chunk3(k, sbase).wait_send()
        return 0
    lax.fori_loop(0, hch, drain3, 0)
    cp_oi.wait()
    cp_ou.wait()
    cp_l.wait()


def solution(mesh):
    def local_fn(mask_blk, user_sh, item_sh, triples):
        n_usr, n_itm = mask_blk.shape
        dim = user_sh.shape[1]
        n_trip = triples.shape[0]
        nch = n_itm // CH
        half = n_itm // 2
        tri = triples.T.reshape(3, n_trip // 128, 128)
        vm = pltpu.VMEM
        dma = pltpu.SemaphoreType.DMA
        nhome = n_trip // 4
        hrow = nhome // 4
        scratch = [
            vm((NSLOT, n_usr, CH), jnp.int32), vm((n_usr, n_itm), BF16), vm((n_usr, 128), F32),
            vm((nch, CH), F32), vm((nch, CH), F32), vm((1, n_usr), F32), vm((1, n_usr), F32),
            vm((n_usr, 128), F32), vm((nch, CH), F32),
            vm((dim, n_itm), BF16), vm((dim, n_itm), BF16), vm((dim, n_itm), BF16), vm((dim, n_usr), BF16),
            vm((dim, n_itm), F32), vm((dim, n_itm), F32), vm((dim, n_itm), F32), vm((dim, n_itm), F32),
            vm((dim, n_itm), F32), vm((dim, half), F32),
            vm((2 * dim, n_usr), F32), vm((2 * dim, n_usr), F32), vm((dim, n_usr), F32), vm((dim, n_usr), F32),
            vm((dim, n_usr), BF16), vm((dim, n_usr), BF16), vm((dim, half), BF16), vm((dim, n_usr // 2), BF16),
            vm((half + 8, 128), F32), vm((2 * n_usr, 128), F32),
            vm((3, n_trip // 128, 128), jnp.int32), vm((3, n_trip // 128, 128), jnp.int32),
            pltpu.SMEM((3, n_trip // 128, 128), jnp.int32),
            vm((5, hrow, 128), F32), vm((3, hrow, 128), F32),
            vm((nhome // 128, 128), F32), vm((7, nhome // 128, 128), F32), vm((n_trip // 128, 128), F32),
            dma((NSLOT,)), dma((3,)), dma((7,)), dma((7,)),
            dma((nch,)), dma((nch,)), dma((nch,)), dma((nch,)), dma((nch // 2,)), dma((nch // 2,)),
            dma((3, hrow // 128)), dma((3, hrow // 128)), dma((7,)), dma((7,)),
        ]
        any_spec = pl.BlockSpec(memory_space=pl.ANY)
        ou, oi, loss = pl.pallas_call(
            functools.partial(kernel, n_usr, n_itm, dim, n_trip),
            out_shape=(jax.ShapeDtypeStruct((dim, n_usr // 2), BF16),
                       jax.ShapeDtypeStruct((dim, half), BF16),
                       jax.ShapeDtypeStruct((n_trip // 128, 128), F32)),
            in_specs=[any_spec] * 4,
            out_specs=(any_spec,) * 3,
            scratch_shapes=scratch,
            compiler_params=pltpu.CompilerParams(collective_id=0, has_side_effects=True,
                                                 vmem_limit_bytes=62 * 1024 * 1024),
            name="gcn",
        )(mask_blk, user_sh.T, item_sh.T, tri)
        return ou.T, oi.T, loss.reshape(n_trip)

    return jax.shard_map(
        local_fn, mesh=mesh,
        in_specs=(P("row", "col"), P(("row", "col"), "emb"), P(("col", "row"), "emb"), P()),
        out_specs=(P(("row", "col"), "emb"), P(("col", "row"), "emb"), P()),
        check_vma=False)
```

time: 262 us -> 76.7 us (0.29)
  Pallas kernels: 0 us -> 69.8 us
  waiting for transfers between devices: 60.5 us -> 0 us
  matrix products: 59.8 us -> 0 us
  other arithmetic: 47.4 us -> 0 us
  local copies, waits for them, and re-layouts: 51.9 us -> 5.98 us
  blocking collectives: 27.1 us -> 0 us
  between operations: 14.1 us -> 0.64 us
    pallas_call x0 -> x1, Pallas kernels: none -> 69.8 us  [local_fn(): pl.pallas_call(functools.partial(kernel, n_usr, n_itm, dim, n_trip), out_...]
    dot_general x6 -> x0, matrix products: 59.8 us -> none  [the longest x3 35.2 us: local_fn(): user_part = jnp.dot(adj_blk, item_panel, preferred_element_type=jnp.float32)]
    psum x2 -> x0, waiting for transfers between devices: 42.8 us -> none  [the longest x1 38.6 us: bpr_terms(): fetched = lax.psum(fetched, ('row', 'col'))]
    gather x3 -> x0, local copies, waits for them, and re-layouts: 39.2 us -> none  [lookup_rows(): picked = jnp.take(table, jnp.clip(local_ids, 0, own_rows - 1), axis=0)]
    convert_element_type x6 -> x0, other arithmetic: 20.2 us -> none  [the longest x1 13.1 us: norm_adjacency(): (inv_user[:, None] * mask_blk.astype(jnp.float32) * inv_item[None, :]).as...]
    reduce_sum x2 -> x0, other arithmetic: 14.6 us -> none  [the longest x1 13.1 us: norm_adjacency(): deg_user = lax.psum(jnp.sum(mask_blk, axis=1), 'col')]
    reduce_scatter x6 -> x0, waiting for transfers between devices: 14.1 us -> none  [the longest x3 7.69 us: local_fn(): lax.psum_scatter(item_part, 'row', scatter_dimension=0, tiled=True)]
    psum x2 -> x0, blocking collectives: 13.7 us -> none  [the longest x1 8.12 us: bpr_terms(): score = lax.psum(jnp.sum(e_user * (e_pos - e_neg), axis=1), 'emb')]
  transfers between devices with their start and end apart: 11 -> 0, of which waited for: 5 -> 0; matrix products, arithmetic and copies ran while one was open for 36% -> 0% of each run, Pallas kernels for 0% -> 0%
where the time goes in v1:
time: 76.7 us; the launch traced here: 76.4 us
  Pallas kernels  69.8 us (91%)
  local copies, waits for them, and re-layouts  5.98 us (8%)
    pallas_call x1, Pallas kernels, local_fn(): pl.pallas_call(functools.partial(kernel, n_usr, n_itm, dim, n_trip), out_...  69.8 us
    unnamed x4, local copies, waits for them, and re-layouts  5.98 us

profile of v1, /device:TPU:0, one launch (start us, length us, event | category | flops | bytes accessed | tf_op | source)
XLA Modules:
  0.0 76.4 jit_solution(13507897902023838077)
XLA Ops:
  0.6 1.5 %copy.9 = s32[1,3,32,128]{3,2,1,0:T(8,128)} copy(s32[1,3,32,128]{3,1,2,0:T(4,128)} %bitcast.13) | data formatting | bytes 98304
  2.1 69.8 %gcn.1 = (bf16[32,256]{1,0:T(8,128)(2,1)}, bf16[32,8192]{1,0:T(8,128)(2,1)}, f32[32,128]{1,0:T(8,128)}) custom-call(s32[512,16384]{1,0:T(8,128)} %mask_ref.1, bf16[32,256]{1,0:T(8,128)(2,1)} %bitcast.14, bf16[32,8192]{1,0:T(8,128)(2,1)} %bitcast.10, s32[3,32,128]{2,1,0:T(8,128)} %bitcast.12), custom_call_target="tpu_custom_call" | custom-call | tf_op jit(solution)/shard_map/gcn/pallas_call | solution.py:362
  71.9 1.3 %copy.13 = bf16[256,32]{0,1:T(8,128)(2,1)} copy(bf16[256,32]{0,1:T(8,128)(2,1)} %bitcast.16) | data formatting | bytes 32768
  73.2 1.9 %copy.14 = bf16[8192,32]{0,1:T(8,128)(2,1)} copy(bf16[8192,32]{0,1:T(8,128)(2,1)} %bitcast.11) | data formatting | bytes 1048576
  75.1 1.3 %copy.15 = f32[4096]{0:T(1024)} copy(f32[4096]{0:T(1024)} %bitcast.15) | data formatting | bytes 32768

commit v2 on v1

v2 whole, which is shorter than its diff:
```python
import functools

import jax
import jax.numpy as jnp
from jax import lax
from jax.experimental import pallas as pl
from jax.experimental.pallas import tpu as pltpu
from jax.sharding import PartitionSpec as P

NUM_LAYERS = 3
CH = 1024
MC = 512
NSLOT = 6
WIDE = 4096
MESH = pl.DeviceIdType.MESH
F32 = jnp.float32
BF16 = jnp.bfloat16


def remote(src, dst, ssem, rsem, dev):
    return pltpu.make_async_remote_copy(src_ref=src, dst_ref=dst, send_sem=ssem, recv_sem=rsem,
                                        device_id=dev, device_id_type=MESH)


def kernel(n_usr, n_itm, dim, n_trip,
           mask_ref, eu_ref, ei_ref, tri_ref, ou_ref, oi_ref, loss_ref,
           stage, adj, rowacc, degi, degi_r, degu, degu_r, invu, invi,
           it0, it1, it2, ut0, i1p, i1r, i2p, i2r,
           up, up_r, u3p, u3_r, uall, sel, oufin, table,
           tri_v, idx_v, idx_t, idx_s, dbuf, drecv, sbuf, srecv, lbuf,
           msem, lsem, ssem, rsem, cs1, cr1, cs2, cr2, cs3, cr3, ds, dr, bs, br, free_sem):
    e = lax.axis_index("emb")
    c = lax.axis_index("col")
    r = lax.axis_index("row")
    sib = {"row": 1 - r}
    xpeer = {"col": 1 - c}
    nch = n_itm // CH
    half = n_itm // 2
    uh = n_usr // 2
    nhome = n_trip // 4
    hrow = nhome // 4

    def mask_copy(j):
        slot = lax.rem(j, NSLOT)
        return pltpu.make_async_copy(mask_ref.at[:, pl.ds(pl.multiple_of(j * MC, MC), MC)], stage.at[slot], msem.at[slot])

    for j in range(NSLOT):
        mask_copy(j).start()
    own_i = it0.at[:, pl.ds(pl.multiple_of(r * half, half), half)]
    own_u = ut0.at[:, pl.ds(pl.multiple_of(c * uh, uh), uh)]
    cp_i = pltpu.make_async_copy(ei_ref, own_i, lsem.at[0])
    cp_u = pltpu.make_async_copy(eu_ref, own_u, lsem.at[1])
    cp_t = pltpu.make_async_copy(tri_ref, tri_v, lsem.at[2])
    cp_i.start()
    cp_u.start()
    cp_t.start()

    barrier = pltpu.get_barrier_semaphore()
    for q in range(1, 8):
        dev = {"emb": lax.rem(e + q // 4, 2), "col": lax.rem(c + (q // 2) % 2, 2), "row": lax.rem(r + q % 2, 2)}
        pl.semaphore_signal(barrier, inc=1, device_id=dev, device_id_type=MESH)

    rowacc[...] = jnp.zeros_like(rowacc)

    def mask_step(j, _):
        slot = lax.rem(j, NSLOT)
        mask_copy(j).wait()
        cols = pl.ds(pl.multiple_of(j * MC, MC), MC)

        def rows_step(g, acc):
            rows = pl.ds(pl.multiple_of(g * 16, 16), 16)
            m = stage[slot, rows, :].astype(F32)
            adj[rows, cols] = m.astype(BF16)
            s = m[:, 0:128]
            for k in range(1, MC // 128):
                s = s + m[:, k * 128:(k + 1) * 128]
            rowacc[rows, :] += s
            return acc + (m[0:8] + m[8:16])

        acc = lax.fori_loop(0, n_usr // 16, rows_step, jnp.zeros((8, MC), F32), unroll=2)
        degi[pl.ds(j, 1), :] = jnp.sum(acc, axis=0, keepdims=True)

        @pl.when(j + NSLOT < n_itm // MC)
        def _():
            mask_copy(j + NSLOT).start()
        return 0

    with jax.named_scope("ph_mask0"):
        lax.fori_loop(0, 8, mask_step, 0)
    cp_i.wait()
    cp_u.wait()
    cp_t.wait()
    with jax.named_scope("ph_barrier"):
        pl.semaphore_wait(barrier, 7)
    rc_i = remote(own_i, own_i, ssem.at[0], rsem.at[0], sib)
    rc_u = remote(own_u, own_u, ssem.at[1], rsem.at[1], xpeer)
    rc_i.start()
    rc_u.start()
    with jax.named_scope("ph_mask1"):
        lax.fori_loop(8, n_itm // MC, mask_step, 0)

    degu[...] = jnp.sum(rowacc[...].T, axis=0, keepdims=True)
    rc_du = remote(degu, degu_r, ssem.at[2], rsem.at[2], xpeer)
    rc_di = remote(degi, degi_r, ssem.at[3], rsem.at[3], sib)
    rc_du.start()
    rc_di.start()

    nrow = n_trip // 128
    idx_v[...] = jnp.zeros_like(idx_v)
    for k in range(3):
        for i in range(nrow):
            idx_v[pl.ds(k * nrow + i, 1), :] = tri_v[pl.ds((k + 1) % 3, 1), i * 128:(i + 1) * 128]
    loc = idx_v[0:2 * nrow, :] - c * n_itm
    idx_v[0:2 * nrow, :] = jnp.where((loc >= 0) & (loc < n_itm), loc, n_itm)
    idx_t[...] = idx_v[...].T
    cp_x = pltpu.make_async_copy(idx_t, idx_s, lsem.at[0])
    cp_x.start()
    table[pl.ds(n_itm, 8), :] = jnp.zeros((8, 128), F32)

    with jax.named_scope("ph_di_wait"):
        rc_di.wait()
    invi[...] = lax.rsqrt(jnp.maximum(degi[...] + degi_r[...], 1.0))
    rc_i.wait()
    rc_u.wait()
    cp_x.wait()
    with jax.named_scope("ph_du_wait"):
        rc_du.wait()
    inv_row = lax.rsqrt(jnp.maximum(degu[...] + degu_r[...], 1.0))
    invu[...] = jnp.broadcast_to(inv_row, (128, n_usr)).T

    def chunk1(j):
        cols = pl.ds(pl.multiple_of(j * CH, CH), CH)
        return remote(i1p.at[:, cols], i1r.at[:, cols], cs1.at[j], cr1.at[j], sib)

    def build_step(i, _):
        for jj in range(2):
            j = i * 2 + jj
            for nt in range(CH // 256):
                cols = pl.ds(pl.multiple_of(j * CH + nt * 256, 256), 256)
                lane = nt * 256 % MC
                wi = jnp.broadcast_to(invi[pl.ds(j * (CH // MC) + nt * 256 // MC, 1), lane:lane + 256], (16, 256))
                part = None
                for kt in range(n_usr // 256):
                    tiles = []
                    for g in range(16):
                        rows = pl.ds(kt * 256 + g * 16, 16)
                        wu = jnp.concatenate([invu[rows, :]] * 2, axis=1)
                        a = (wu * wi).astype(BF16) * adj[rows, cols]
                        adj[rows, cols] = a
                        tiles.append(a)
                    p = jnp.dot(ut0[:, kt * 256:(kt + 1) * 256], jnp.concatenate(tiles, axis=0),
                                preferred_element_type=F32)
                    part = p if part is None else part + p
                i1p[:, cols] = part
        for jj in range(2):
            chunk1(i * 2 + jj).start()
        return 0

    with jax.named_scope("ph_build"):
        lax.fori_loop(0, nch // 2, build_step, 0)

    def dot_t(lhs, a):
        return lax.dot_general(lhs, a, (((1,), (1,)), ((), ())), preferred_element_type=F32)

    up[...] = jnp.zeros_like(up)

    def user_step(i, _):
        cols = pl.ds(pl.multiple_of(i * WIDE, WIDE), WIDE)
        for t in range(WIDE // CH):
            chunk1(i * (WIDE // CH) + t).wait_recv()
        v1 = (i1p[:, cols] + i1r[:, cols]).astype(BF16)
        it1[:, cols] = v1
        lhs = jnp.concatenate([it0[:, cols], v1], axis=0)
        up[...] += dot_t(lhs, adj[:, cols])
        return 0

    with jax.named_scope("ph_user"):
        lax.fori_loop(0, n_itm // WIDE, user_step, 0)
    rc_up = remote(up, up_r, ssem.at[4], rsem.at[4], xpeer)
    rc_up.start()
    pl.semaphore_signal(free_sem, inc=1, device_id=sib, device_id_type=MESH)

    def sent1(j, _):
        chunk1(j).wait_send()
        return 0
    lax.fori_loop(0, nch, sent1, 0)
    home = c * 2 + r

    def sel_step(g, _):
        users = lax.broadcasted_iota(jnp.int32, (16, 128), 0) + g * 16
        for t in range(nhome // 128):
            ids = idx_v[pl.ds(2 * nrow + home * (nhome // 128) + t, 1), :]
            hit = jnp.where(users == jnp.broadcast_to(ids, (16, 128)), 1.0, 0.0)
            sel[pl.ds(pl.multiple_of(g * 16, 16), 16), t * 128:(t + 1) * 128] = hit.astype(BF16)
        return 0

    with jax.named_scope("ph_sel"):
        lax.fori_loop(0, 2 * n_usr // 16, sel_step, 0, unroll=2)
    with jax.named_scope("ph_up_wait"):
        rc_up.wait()
    u12 = (up[...] + up_r[...]).astype(BF16)

    def chunk2(j):
        cols = pl.ds(pl.multiple_of(j * CH, CH), CH)
        return remote(i2p.at[:, cols], i2r.at[:, cols], cs2.at[j], cr2.at[j], sib)

    def chunk3(j):
        cols = pl.ds(pl.multiple_of(j * CH, CH), CH)
        return remote(i1p.at[:, cols], i1r.at[:, cols], cs3.at[j], cr3.at[j], sib)

    nw = WIDE // CH

    def item_step(i, _):
        cols = pl.ds(pl.multiple_of(i * WIDE, WIDE), WIDE)
        part = jnp.dot(u12, adj[:, cols], preferred_element_type=F32)
        i2p[:, cols] = part[0:dim]
        i1p[:, cols] = part[dim:2 * dim]
        for t in range(nw):
            chunk2(i * nw + t).start()
        return 0

    def send3(j, _):
        chunk3(j).start()
        return 0

    with jax.named_scope("ph_item"):
        lax.fori_loop(0, n_itm // WIDE, item_step, 0)
        pl.semaphore_wait(free_sem, 1)
        lax.fori_loop(0, nch, send3, 0)

    u3p[...] = jnp.zeros_like(u3p)

    def user3_step(i, _):
        cols = pl.ds(pl.multiple_of(i * WIDE, WIDE), WIDE)
        for t in range(nw):
            chunk2(i * nw + t).wait_recv()
        v2 = (i2p[:, cols] + i2r[:, cols]).astype(BF16)
        it2[:, cols] = v2
        u3p[...] += dot_t(v2, adj[:, cols])
        return 0

    with jax.named_scope("ph_user3"):
        lax.fori_loop(0, n_itm // WIDE, user3_step, 0)
    rc_u3 = remote(u3p, u3_r, ssem.at[5], rsem.at[5], xpeer)
    rc_u3.start()

    def final_step(k, _):
        cols = pl.ds(pl.multiple_of(k * CH, CH), CH)
        chunk3(k).wait_recv()
        v3 = (i1p[:, cols] + i1r[:, cols]).astype(BF16)
        acc = it0[:, cols].astype(F32) + it1[:, cols].astype(F32)
        acc = (acc + it2[:, cols].astype(F32)) + v3.astype(F32)
        fin = (acc * (1.0 / (NUM_LAYERS + 1))).astype(BF16)
        it1[:, cols] = fin
        fin = fin.astype(F32)
        for b in range(CH // 128):
            blk = fin[:, b * 128:(b + 1) * 128]
            table[pl.ds(pl.multiple_of(k * CH + b * 128, 128), 128), :] = jnp.concatenate([blk] * 4, axis=0).T
        return 0

    with jax.named_scope("ph_final"):
        lax.fori_loop(0, nch, final_step, 0)
    cp_oi = pltpu.make_async_copy(it1.at[:, pl.ds(pl.multiple_of(r * half, half), half)], oi_ref, lsem.at[1])
    cp_oi.start()

    lane_blk = lax.broadcasted_iota(jnp.int32, (1, 128), 1) // dim

    def pack(rows4):
        d = rows4[0]
        for b in range(1, 4):
            d = jnp.where(lane_blk == b, rows4[b], d)
        return d

    def d_send(ah):
        rows = pl.ds(pl.multiple_of(ah * 128, 128), 128)
        return remote(dbuf.at[1, rows, :], drecv.at[rows, :], ds.at[ah], dr.at[ah], xpeer)

    def diff_rows(q, ah):
        first = (lax.rem(c + q, 2) * 2 + r) * (nhome // 128) + ah

        def body(al, _):
            out = []
            for b in range(4):
                row = first + b * (hrow // 128)
                p = idx_s[al, row]
                n = idx_s[al, nrow + row]
                out.append(table[pl.ds(p, 1), :] - table[pl.ds(n, 1), :])
            dbuf[q, pl.ds(pl.multiple_of(ah * 128, 128) + al, 1), :] = pack(out)
            return 0

        lax.fori_loop(0, 128, body, 0, unroll=8)

    def diff_send(ah, _):
        diff_rows(1, ah)
        d_send(ah).start()
        return 0

    def diff_keep(ah, _):
        diff_rows(0, ah)
        return 0

    with jax.named_scope("ph_diff"):
        lax.fori_loop(0, hrow // 128, diff_send, 0)
    with jax.named_scope("ph_diff"):
        lax.fori_loop(0, hrow // 128, diff_keep, 0)

    with jax.named_scope("ph_u3_wait"):
        rc_u3.wait()
    u3 = (u3p[...] + u3_r[...]).astype(BF16).astype(F32)
    uacc = ut0[...].astype(F32) + u12[0:dim].astype(F32)
    uacc = (uacc + u12[dim:2 * dim].astype(F32)) + u3
    fin_u = (uacc * (1.0 / (NUM_LAYERS + 1))).astype(BF16)
    own_cols = pl.ds(pl.multiple_of(r * n_usr, n_usr), n_usr)
    uall[:, own_cols] = fin_u
    rc_uf = remote(uall.at[:, own_cols], uall.at[:, own_cols], ssem.at[6], rsem.at[6], sib)
    rc_uf.start()
    oufin[...] = uall[:, pl.ds(pl.multiple_of(r * n_usr + c * uh, uh), uh)]
    cp_ou = pltpu.make_async_copy(oufin, ou_ref, lsem.at[2])
    cp_ou.start()
    with jax.named_scope("ph_uf_wait"):
        rc_uf.wait()
    urow = jnp.dot(uall[...], sel[...], preferred_element_type=F32)

    with jax.named_scope("ph_d_wait"):
        for ah in range(hrow // 128):
            d_send(ah).wait()
    dsum = (dbuf[0] + drecv[...]).T
    for b in range(4):
        prod = dsum[b * dim:(b + 1) * dim, :] * urow[:, b * hrow:(b + 1) * hrow]
        s = jnp.sum(prod, axis=0, keepdims=True)
        for h in range(hrow // 128):
            sbuf[pl.ds(b * (hrow // 128) + h, 1), :] = s[:, h * 128:(h + 1) * 128]

    def s_send(q):
        dev = {"emb": lax.rem(e + q // 4, 2), "col": lax.rem(c + (q // 2) % 2, 2), "row": lax.rem(r + q % 2, 2)}
        return remote(sbuf, srecv.at[q - 1], bs.at[q - 1], br.at[q - 1], dev)

    for q in range(7, 0, -1):
        s_send(q).start()
    with jax.named_scope("ph_s_wait"):
        for q in range(7, 0, -1):
            s_send(q).wait()
    for q in range(4):
        own = sbuf[...] if q == 0 else srecv[q - 1]
        x = own + srecv[q + 3]
        hq = lax.rem(c + q // 2, 2) * 2 + lax.rem(r + q % 2, 2)
        ls = jnp.maximum(-x, 0.0) + jnp.log1p(jnp.exp(-jnp.abs(x)))
        lbuf[pl.ds(pl.multiple_of(hq * (nhome // 128), 8), nhome // 128), :] = ls
    cp_l = pltpu.make_async_copy(lbuf, loss_ref, lsem.at[0])
    cp_l.start()

    def drain(j, _):
        chunk2(j).wait_send()
        chunk3(j).wait_send()
        return 0
    with jax.named_scope("ph_drain"):
        lax.fori_loop(0, nch, drain, 0)

    cp_oi.wait()
    cp_ou.wait()
    cp_l.wait()


def solution(mesh):
    def local_fn(mask_blk, user_sh, item_sh, triples):
        n_usr, n_itm = mask_blk.shape
        dim = user_sh.shape[1]
        n_trip = triples.shape[0]
        nch = n_itm // CH
        half = n_itm // 2
        tri = triples.T
        vm = pltpu.VMEM
        dma = pltpu.SemaphoreType.DMA
        nhome = n_trip // 4
        hrow = nhome // 4
        scratch = [
            vm((NSLOT, n_usr, MC), jnp.int32), vm((n_usr, n_itm), BF16), vm((n_usr, 128), F32),
            vm((n_itm // MC, MC), F32), vm((n_itm // MC, MC), F32), vm((1, n_usr), F32), vm((1, n_usr), F32),
            vm((n_usr, 128), F32), vm((n_itm // MC, MC), F32),
            vm((dim, n_itm), BF16), vm((dim, n_itm), BF16), vm((dim, n_itm), BF16), vm((dim, n_usr), BF16),
            vm((dim, n_itm), F32), vm((dim, n_itm), F32), vm((dim, n_itm), F32), vm((dim, n_itm), F32),
            vm((2 * dim, n_usr), F32), vm((2 * dim, n_usr), F32), vm((dim, n_usr), F32), vm((dim, n_usr), F32),
            vm((dim, 2 * n_usr), BF16), vm((2 * n_usr, nhome), BF16), vm((dim, n_usr // 2), BF16),
            vm((n_itm + 8, 128), F32),
            vm((3, n_trip), jnp.int32), vm((128, 128), jnp.int32), vm((128, 128), jnp.int32),
            pltpu.SMEM((128, 128), jnp.int32),
            vm((2, hrow, 128), F32), vm((hrow, 128), F32),
            vm((nhome // 128, 128), F32), vm((7, nhome // 128, 128), F32), vm((n_trip // 128, 128), F32),
            dma((NSLOT,)), dma((3,)), dma((7,)), dma((7,)),
            dma((nch,)), dma((nch,)), dma((nch,)), dma((nch,)), dma((nch,)), dma((nch,)),
            dma((hrow // 128,)), dma((hrow // 128,)), dma((7,)), dma((7,)), pltpu.SemaphoreType.REGULAR,
        ]
        any_spec = pl.BlockSpec(memory_space=pl.ANY)
        ou, oi, loss = pl.pallas_call(
            functools.partial(kernel, n_usr, n_itm, dim, n_trip),
            out_shape=(jax.ShapeDtypeStruct((dim, n_usr // 2), BF16),
                       jax.ShapeDtypeStruct((dim, half), BF16),
                       jax.ShapeDtypeStruct((n_trip // 128, 128), F32)),
            in_specs=[any_spec] * 4,
            out_specs=(any_spec,) * 3,
            scratch_shapes=scratch,
            compiler_params=pltpu.CompilerParams(collective_id=0, has_side_effects=True,
                                                 vmem_limit_bytes=62 * 1024 * 1024),
            name="gcn",
        )(mask_blk, user_sh.T, item_sh.T, tri)
        return ou.T, oi.T, loss.reshape(n_trip)

    return jax.shard_map(
        local_fn, mesh=mesh,
        in_specs=(P("row", "col"), P(("row", "col"), "emb"), P(("col", "row"), "emb"), P()),
        out_specs=(P(("row", "col"), "emb"), P(("col", "row"), "emb"), P()),
        check_vma=False)
```

time: 76.7 us -> 63.8 us (0.83)
  Pallas kernels: 69.8 us -> 58.3 us
  local copies, waits for them, and re-layouts: 5.98 us -> 4.51 us
    pallas_call x1, Pallas kernels: 69.8 us -> 58.3 us  [local_fn(): pl.pallas_call(functools.partial(kernel, n_usr, n_itm, dim, n_trip), out_...]
    unnamed x4 -> x3, local copies, waits for them, and re-layouts: 5.98 us -> 4.51 us
where the time goes in v2:
time: 63.8 us; the launch traced here: 63.5 us
  Pallas kernels  58.3 us (91%)
  local copies, waits for them, and re-layouts  4.51 us (7%)
  between operations  0.64 us (1%)
    pallas_call x1, Pallas kernels, local_fn(): pl.pallas_call(functools.partial(kernel, n_usr, n_itm, dim, n_trip), out_...  58.3 us
    unnamed x3, local copies, waits for them, and re-layouts  4.51 us

profile of v2, /device:TPU:0, one launch (start us, length us, event | category | flops | bytes accessed | tf_op | source)
XLA Modules:
  0.0 63.5 jit_solution(9672640683632762905)
XLA Ops:
  0.6 58.3 %gcn.1 = (bf16[32,256]{1,0:T(8,128)(2,1)}, bf16[32,8192]{1,0:T(8,128)(2,1)}, f32[32,128]{1,0:T(8,128)}) custom-call(s32[512,16384]{1,0:T(8,128)} %mask_ref.1, bf16[32,256]{1,0:T(8,128)(2,1)} %bitcast.9, bf16[32,8192]{1,0:T(8,128)(2,1)} %bitcast.6, s32[3,4096]{1,0:T(4,128)} %bitcast.8), custom_call_target="tpu_custom_call" | custom-call | tf_op jit(solution)/shard_map/gcn/pallas_call | solution.py:394
  59.0 1.3 %copy.10 = bf16[256,32]{0,1:T(8,128)(2,1)} copy(bf16[256,32]{0,1:T(8,128)(2,1)} %bitcast.11) | data formatting | bytes 32768
  60.3 1.9 %copy.11 = bf16[8192,32]{0,1:T(8,128)(2,1)} copy(bf16[8192,32]{0,1:T(8,128)(2,1)} %bitcast.7) | data formatting | bytes 1048576
  62.2 1.3 %copy.12 = f32[4096]{0:T(1024)} copy(f32[4096]{0:T(1024)} %bitcast.10) | data formatting | bytes 32768

commit v3 on v2

--- a/solution.py
+++ b/solution.py
@@ -26,8 +26,8 @@
            mask_ref, eu_ref, ei_ref, tri_ref, ou_ref, oi_ref, loss_ref,
            stage, adj, rowacc, degi, degi_r, degu, degu_r, invu, invi,
            it0, it1, it2, ut0, i1p, i1r, i2p, i2r,
-           up, up_r, u3p, u3_r, uall, sel, oufin, table,
-           tri_v, idx_v, idx_t, idx_s, dbuf, drecv, sbuf, srecv, lbuf,
+           up, up_r, u3p, u3_r, uall, sel, table,
+           tri_v, idx_v, idx_t, idx_s, dbuf, drecv, sbuf, srecv,
            msem, lsem, ssem, rsem, cs1, cr1, cs2, cr2, cs3, cr3, ds, dr, bs, br, free_sem):
     e = lax.axis_index("emb")
     c = lax.axis_index("col")
@@ -105,13 +105,23 @@
     rc_du.start()
     rc_di.start()
 
-    nrow = n_trip // 128
+    def tri_row(k, row):
+        return tri_v[pl.ds(k, 1), pl.ds(pl.multiple_of(row * 128, 128), 128)]
+
+    def home_row(q):
+        return (lax.rem(c + q, 2) * 2 + r) * (nhome // 128)
+
+    nah = hrow // 128
+    ncol = 8 * nah
     idx_v[...] = jnp.zeros_like(idx_v)
-    for k in range(3):
-        for i in range(nrow):
-            idx_v[pl.ds(k * nrow + i, 1), :] = tri_v[pl.ds((k + 1) % 3, 1), i * 128:(i + 1) * 128]
-    loc = idx_v[0:2 * nrow, :] - c * n_itm
-    idx_v[0:2 * nrow, :] = jnp.where((loc >= 0) & (loc < n_itm), loc, n_itm)
+    for k in range(2):
+        for q in range(2):
+            for ah in range(nah):
+                for b in range(4):
+                    col = k * ncol + (q * nah + ah) * 4 + b
+                    idx_v[pl.ds(col, 1), :] = tri_row(k + 1, home_row(q) + b * nah + ah)
+    loc = idx_v[0:2 * ncol, :] - c * n_itm
+    idx_v[0:2 * ncol, :] = jnp.where((loc >= 0) & (loc < n_itm), loc, n_itm)
     idx_t[...] = idx_v[...].T
     cp_x = pltpu.make_async_copy(idx_t, idx_s, lsem.at[0])
     cp_x.start()
@@ -184,12 +194,10 @@
         chunk1(j).wait_send()
         return 0
     lax.fori_loop(0, nch, sent1, 0)
-    home = c * 2 + r
-
     def sel_step(g, _):
         users = lax.broadcasted_iota(jnp.int32, (16, 128), 0) + g * 16
         for t in range(nhome // 128):
-            ids = idx_v[pl.ds(2 * nrow + home * (nhome // 128) + t, 1), :]
+            ids = tri_row(0, home_row(0) + t)
             hit = jnp.where(users == jnp.broadcast_to(ids, (16, 128)), 1.0, 0.0)
             sel[pl.ds(pl.multiple_of(g * 16, 16), 16), t * 128:(t + 1) * 128] = hit.astype(BF16)
         return 0
@@ -260,8 +268,7 @@
 
     with jax.named_scope("ph_final"):
         lax.fori_loop(0, nch, final_step, 0)
-    cp_oi = pltpu.make_async_copy(it1.at[:, pl.ds(pl.multiple_of(r * half, half), half)], oi_ref, lsem.at[1])
-    cp_oi.start()
+    oi_ref[...] = it1[:, pl.ds(pl.multiple_of(r * half, half), half)]
 
     lane_blk = lax.broadcasted_iota(jnp.int32, (1, 128), 1) // dim
 
@@ -276,33 +283,25 @@
         return remote(dbuf.at[1, rows, :], drecv.at[rows, :], ds.at[ah], dr.at[ah], xpeer)
 
     def diff_rows(q, ah):
-        first = (lax.rem(c + q, 2) * 2 + r) * (nhome // 128) + ah
-
         def body(al, _):
             out = []
             for b in range(4):
-                row = first + b * (hrow // 128)
-                p = idx_s[al, row]
-                n = idx_s[al, nrow + row]
+                col = (q * nah + ah) * 4 + b
+                p = idx_s[al, col]
+                n = idx_s[al, ncol + col]
                 out.append(table[pl.ds(p, 1), :] - table[pl.ds(n, 1), :])
-            dbuf[q, pl.ds(pl.multiple_of(ah * 128, 128) + al, 1), :] = pack(out)
+            dbuf[q, pl.ds(ah * 128 + al, 1), :] = pack(out)
             return 0
 
         lax.fori_loop(0, 128, body, 0, unroll=8)
 
-    def diff_send(ah, _):
-        diff_rows(1, ah)
-        d_send(ah).start()
-        return 0
-
-    def diff_keep(ah, _):
-        diff_rows(0, ah)
-        return 0
-
     with jax.named_scope("ph_diff"):
-        lax.fori_loop(0, hrow // 128, diff_send, 0)
+        for ah in range(nah):
+            diff_rows(1, ah)
+            d_send(ah).start()
     with jax.named_scope("ph_diff"):
-        lax.fori_loop(0, hrow // 128, diff_keep, 0)
+        for ah in range(nah):
+            diff_rows(0, ah)
 
     with jax.named_scope("ph_u3_wait"):
         rc_u3.wait()
@@ -314,9 +313,7 @@
     uall[:, own_cols] = fin_u
     rc_uf = remote(uall.at[:, own_cols], uall.at[:, own_cols], ssem.at[6], rsem.at[6], sib)
     rc_uf.start()
-    oufin[...] = uall[:, pl.ds(pl.multiple_of(r * n_usr + c * uh, uh), uh)]
-    cp_ou = pltpu.make_async_copy(oufin, ou_ref, lsem.at[2])
-    cp_ou.start()
+    ou_ref[...] = uall[:, pl.ds(pl.multiple_of(r * n_usr + c * uh, uh), uh)]
     with jax.named_scope("ph_uf_wait"):
         rc_uf.wait()
     urow = jnp.dot(uall[...], sel[...], preferred_element_type=F32)
@@ -345,9 +342,7 @@
         x = own + srecv[q + 3]
         hq = lax.rem(c + q // 2, 2) * 2 + lax.rem(r + q % 2, 2)
         ls = jnp.maximum(-x, 0.0) + jnp.log1p(jnp.exp(-jnp.abs(x)))
-        lbuf[pl.ds(pl.multiple_of(hq * (nhome // 128), 8), nhome // 128), :] = ls
-    cp_l = pltpu.make_async_copy(lbuf, loss_ref, lsem.at[0])
-    cp_l.start()
+        loss_ref[pl.ds(pl.multiple_of(hq * (nhome // 128), 8), nhome // 128), :] = ls
 
     def drain(j, _):
         chunk2(j).wait_send()
@@ -356,9 +351,14 @@
     with jax.named_scope("ph_drain"):
         lax.fori_loop(0, nch, drain, 0)
 
-    cp_oi.wait()
-    cp_ou.wait()
-    cp_l.wait()
+
+def store_kernel(*refs):
+    srcs, dsts, sem = refs[0:3], refs[3:6], refs[6]
+    copies = [pltpu.make_async_copy(a, b, sem.at[k]) for k, (a, b) in enumerate(zip(srcs, dsts))]
+    for copy in copies:
+        copy.start()
+    for copy in copies:
+        copy.wait()
 
 
 def solution(mesh):
@@ -380,29 +380,39 @@
             vm((dim, n_itm), BF16), vm((dim, n_itm), BF16), vm((dim, n_itm), BF16), vm((dim, n_usr), BF16),
             vm((dim, n_itm), F32), vm((dim, n_itm), F32), vm((dim, n_itm), F32), vm((dim, n_itm), F32),
             vm((2 * dim, n_usr), F32), vm((2 * dim, n_usr), F32), vm((dim, n_usr), F32), vm((dim, n_usr), F32),
-            vm((dim, 2 * n_usr), BF16), vm((2 * n_usr, nhome), BF16), vm((dim, n_usr // 2), BF16),
+            vm((dim, 2 * n_usr), BF16), vm((2 * n_usr, nhome), BF16),
             vm((n_itm + 8, 128), F32),
             vm((3, n_trip), jnp.int32), vm((128, 128), jnp.int32), vm((128, 128), jnp.int32),
             pltpu.SMEM((128, 128), jnp.int32),
             vm((2, hrow, 128), F32), vm((hrow, 128), F32),
-            vm((nhome // 128, 128), F32), vm((7, nhome // 128, 128), F32), vm((n_trip // 128, 128), F32),
+            vm((nhome // 128, 128), F32), vm((7, nhome // 128, 128), F32),
             dma((NSLOT,)), dma((3,)), dma((7,)), dma((7,)),
             dma((nch,)), dma((nch,)), dma((nch,)), dma((nch,)), dma((nch,)), dma((nch,)),
             dma((hrow // 128,)), dma((hrow // 128,)), dma((7,)), dma((7,)), pltpu.SemaphoreType.REGULAR,
         ]
-        any_spec = pl.BlockSpec(memory_space=pl.ANY)
+        hbm_spec = pl.BlockSpec(memory_space=pltpu.HBM)
+        vmem_spec = pl.BlockSpec(memory_space=pltpu.VMEM)
         ou, oi, loss = pl.pallas_call(
             functools.partial(kernel, n_usr, n_itm, dim, n_trip),
             out_shape=(jax.ShapeDtypeStruct((dim, n_usr // 2), BF16),
                        jax.ShapeDtypeStruct((dim, half), BF16),
                        jax.ShapeDtypeStruct((n_trip // 128, 128), F32)),
-            in_specs=[any_spec] * 4,
-            out_specs=(any_spec,) * 3,
+            in_specs=[hbm_spec] * 4,
+            out_specs=(vmem_spec,) * 3,
             scratch_shapes=scratch,
             compiler_params=pltpu.CompilerParams(collective_id=0, has_side_effects=True,
-                                                 vmem_limit_bytes=62 * 1024 * 1024),
+                                                 vmem_limit_bytes=50 * 1024 * 1024),
             name="gcn",
-        )(mask_blk, user_sh.T, item_sh.T, tri)
+        )(mask_blk, *[pltpu.with_memory_space_constraint(v, pltpu.HBM) for v in (user_sh.T, item_sh.T, tri)])
+        ou, oi, loss = pl.pallas_call(
+            store_kernel,
+            out_shape=tuple(jax.ShapeDtypeStruct(v.shape, v.dtype) for v in (ou, oi, loss)),
+            in_specs=[vmem_spec] * 3,
+            out_specs=(pl.BlockSpec(memory_space=pl.ANY),) * 3,
+            scratch_shapes=[dma((3,))],
+            compiler_params=pltpu.CompilerParams(vmem_limit_bytes=4 * 1024 * 1024),
+            name="store",
+        )(ou, oi, loss)
         return ou.T, oi.T, loss.reshape(n_trip)
 
     return jax.shard_map(

time: 63.8 us -> 55.5 us (0.87)
  local copies, waits for them, and re-layouts: 4.51 us -> 0 us
  Pallas kernels: 58.3 us -> 54.8 us
    unnamed x3 -> x0, local copies, waits for them, and re-layouts: 4.51 us -> none
    pallas_call x1, Pallas kernels: 58.3 us -> 53.9 us  [local_fn(): pl.pallas_call(functools.partial(kernel, n_usr, n_itm, dim, n_trip), out_...]
    pallas_call x0 -> x1, Pallas kernels: none -> 0.83 us  [local_fn(): pl.pallas_call(store_kernel, out_shape=tuple((jax.ShapeDtypeStruct(v.shap...]
where the time goes in v3:
time: 55.5 us; the launch traced here: 55.4 us
  Pallas kernels  54.8 us (99%)
  between operations  0.64 us (1%)
    pallas_call x1, Pallas kernels, local_fn(): pl.pallas_call(functools.partial(kernel, n_usr, n_itm, dim, n_trip), out_...  53.9 us

profile of v3, /device:TPU:0, one launch (start us, length us, event | category | flops | bytes accessed | tf_op | source)
XLA Modules:
  0.0 55.4 jit_solution(11667695036934903025)
XLA Ops:
  0.6 53.9 %gcn.1 = (bf16[32,256]{1,0:T(8,128)(2,1)S(1)}, bf16[32,8192]{1,0:T(8,128)(2,1)S(1)}, f32[32,128]{1,0:T(8,128)S(1)}) custom-call(s32[512,16384]{1,0:T(8,128)} %mask_ref.1, bf16[32,256]{1,0:T(8,128)(2,1)} %bitcast.8, bf16[32,8192]{1,0:T(8,128)(2,1)} %bitcast.6, s32[3,4096]{1,0:T(4,128)} %bitcast.7), custom_call_target="tpu_custom_call" | custom-call | tf_op jit(solution)/shard_map/gcn/pallas_call | solution.py:395
  54.6 0.8 %store.1 = (bf16[32,256]{1,0:T(8,128)(2,1)}, bf16[32,8192]{1,0:T(8,128)(2,1)}, f32[32,128]{1,0:T(8,128)}) custom-call(bf16[32,256]{1,0:T(8,128)(2,1)S(1)} %get-tuple-element.9.refs_0_, bf16[32,8192]{1,0:T(8,128)(2,1)S(1)} %get-tuple-element.10.refs_1_, f32[32,128]{1,0:T(8,128)S(1)} %get-tuple-element.11.refs_2_), custom_call_target="tpu_custom_call" | custom-call | tf_op jit(solution)/shard_map/store/pallas_call | solution.py:407

commit v4 on v3

v4 whole, which is shorter than its diff:
```python
import functools

import jax
import jax.numpy as jnp
from jax import lax
from jax.experimental import pallas as pl
from jax.experimental.pallas import tpu as pltpu
from jax.sharding import PartitionSpec as P

NUM_LAYERS = 3
CH = 2048
MC = 512
NSLOT = 6
FIN = 4096
WIDE = 8192
NARROW = 4096
MESH = pl.DeviceIdType.MESH
F32 = jnp.float32
BF16 = jnp.bfloat16


def remote(src, dst, ssem, rsem, dev):
    return pltpu.make_async_remote_copy(src_ref=src, dst_ref=dst, send_sem=ssem, recv_sem=rsem,
                                        device_id=dev, device_id_type=MESH)


def kernel(n_usr, n_itm, dim, n_trip,
           mask_ref, eu_ref, ei_ref, tri_ref, ou_ref, oi_ref, loss_ref,
           stage, adj, rowacc, degi, degi_r, degu, degu_r, invu, invi,
           it0, it1, it2, ut0, i1p, i1r, i2p, i2r,
           up, up_r, u3p, u3_r, uall, sel, table,
           tri_v, idx_v, idx_t, idx_s, dbuf, dt, drecv, sbuf, srecv,
           msem, lsem, ssem, rsem, cs1, cr1, cs2, cr2, ds, dr, bs, br, free_sem):
    e = lax.axis_index("emb")
    c = lax.axis_index("col")
    r = lax.axis_index("row")
    sib = {"row": 1 - r}
    xpeer = {"col": 1 - c}
    nch = n_itm // CH
    half = n_itm // 2
    uh = n_usr // 2
    nhome = n_trip // 4
    hrow = nhome // 4

    def mask_copy(j):
        slot = lax.rem(j, NSLOT)
        return pltpu.make_async_copy(mask_ref.at[:, pl.ds(pl.multiple_of(j * MC, MC), MC)], stage.at[slot], msem.at[slot])

    for j in range(NSLOT):
        mask_copy(j).start()
    own_i = it0.at[:, pl.ds(pl.multiple_of(r * half, half), half)]
    own_u = ut0.at[:, pl.ds(pl.multiple_of(c * uh, uh), uh)]
    cp_i = pltpu.make_async_copy(ei_ref, own_i, lsem.at[0])
    cp_u = pltpu.make_async_copy(eu_ref, own_u, lsem.at[1])
    cp_t = pltpu.make_async_copy(tri_ref, tri_v, lsem.at[2])
    cp_i.start()
    cp_u.start()
    cp_t.start()

    barrier = pltpu.get_barrier_semaphore()
    for q in range(1, 8):
        dev = {"emb": lax.rem(e + q // 4, 2), "col": lax.rem(c + (q // 2) % 2, 2), "row": lax.rem(r + q % 2, 2)}
        pl.semaphore_signal(barrier, inc=1, device_id=dev, device_id_type=MESH)

    rowacc[...] = jnp.zeros_like(rowacc)

    def mask_step(j, _):
        slot = lax.rem(j, NSLOT)
        mask_copy(j).wait()
        cols = pl.ds(pl.multiple_of(j * MC, MC), MC)

        def rows_step(g, acc):
            rows = pl.ds(pl.multiple_of(g * 16, 16), 16)
            m = stage[slot, rows, :].astype(F32)
            adj[rows, cols] = m.astype(BF16)
            s = m[:, 0:128]
            for k in range(1, MC // 128):
                s = s + m[:, k * 128:(k + 1) * 128]
            rowacc[rows, :] += s
            return acc + (m[0:8] + m[8:16])

        acc = lax.fori_loop(0, n_usr // 16, rows_step, jnp.zeros((8, MC), F32), unroll=2)
        degi[pl.ds(j, 1), :] = jnp.sum(acc, axis=0, keepdims=True)

        @pl.when(j + NSLOT < n_itm // MC)
        def _():
            mask_copy(j + NSLOT).start()
        return 0

    with jax.named_scope("ph_mask0"):
        lax.fori_loop(0, 8, mask_step, 0)
    cp_i.wait()
    cp_u.wait()
    cp_t.wait()
    with jax.named_scope("ph_barrier"):
        pl.semaphore_wait(barrier, 7)
    rc_i = remote(own_i, own_i, ssem.at[0], rsem.at[0], sib)
    rc_u = remote(own_u, own_u, ssem.at[1], rsem.at[1], xpeer)
    rc_i.start()
    rc_u.start()
    with jax.named_scope("ph_mask1"):
        lax.fori_loop(8, n_itm // MC, mask_step, 0)

    degu[...] = jnp.sum(rowacc[...].T, axis=0, keepdims=True)
    rc_du = remote(degu, degu_r, ssem.at[2], rsem.at[2], xpeer)
    rc_di = remote(degi, degi_r, ssem.at[3], rsem.at[3], sib)
    rc_du.start()
    rc_di.start()

    def tri_row(k, row):
        return tri_v[pl.ds(k, 1), pl.ds(pl.multiple_of(row * 128, 128), 128)]

    def home_row(q):
        return (lax.rem(c + q, 2) * 2 + r) * (nhome // 128)

    nrow = nhome // 128
    ncol = 2 * nrow
    idx_v[...] = jnp.zeros_like(idx_v)
    for k in range(2):
        for q in range(2):
            for row in range(nrow):
                idx_v[pl.ds(k * ncol + q * nrow + row, 1), :] = tri_row(k + 1, home_row(q) + row)
    loc = idx_v[0:2 * ncol, :] - c * n_itm
    idx_v[0:2 * ncol, :] = jnp.where((loc >= 0) & (loc < n_itm), loc, n_itm)
    idx_t[...] = idx_v[...].T
    cp_x = pltpu.make_async_copy(idx_t, idx_s, lsem.at[0])
    cp_x.start()
    table[pl.ds(n_itm, 8), :] = jnp.zeros((8, dim), F32)

    with jax.named_scope("ph_di_wait"):
        rc_di.wait()
    invi[...] = lax.rsqrt(jnp.maximum(degi[...] + degi_r[...], 1.0))
    rc_i.wait()
    rc_u.wait()
    cp_x.wait()
    with jax.named_scope("ph_du_wait"):
        rc_du.wait()
    inv_row = lax.rsqrt(jnp.maximum(degu[...] + degu_r[...], 1.0))
    invu[...] = jnp.broadcast_to(inv_row, (128, n_usr)).T

    nst = n_itm // WIDE

    def chunk1(j):
        cols = pl.ds(pl.multiple_of(j * CH, CH), CH)
        return remote(i1p.at[:, cols], i1r.at[:, cols], cs1, cr1.at[j // (WIDE // CH)], sib)

    def step1(i):
        cols = pl.ds(pl.multiple_of(i * WIDE, WIDE), WIDE)
        return remote(i1p.at[:, cols], i1r.at[:, cols], cs1, cr1.at[i], sib)

    def build_step(j, _):
        for nt in range(CH // 256):
            cols = pl.ds(pl.multiple_of(j * CH + nt * 256, 256), 256)
            lane = nt * 256 % MC
            wi = jnp.broadcast_to(invi[pl.ds(j * (CH // MC) + nt * 256 // MC, 1), lane:lane + 256], (16, 256))
            part = None
            for kt in range(n_usr // 256):
                tiles = []
                for g in range(16):
                    rows = pl.ds(kt * 256 + g * 16, 16)
                    wu = jnp.concatenate([invu[rows, :]] * 2, axis=1)
                    a = (wu * wi).astype(BF16) * adj[rows, cols]
                    adj[rows, cols] = a
                    tiles.append(a)
                p = jnp.dot(ut0[:, kt * 256:(kt + 1) * 256], jnp.concatenate(tiles, axis=0),
                            preferred_element_type=F32)
                part = p if part is None else part + p
            i1p[:, cols] = part
        chunk1(j).start()
        return 0

    with jax.named_scope("ph_build"):
        lax.fori_loop(0, nch, build_step, 0)

    def dot_t(a, b):
        return lax.dot_general(a, b, (((1,), (1,)), ((), ())), preferred_element_type=F32)

    up[...] = jnp.zeros_like(up)
    rc_up = []
    for h in range(2):
        rows = pl.ds(h * uh, uh)

        def user_step(i, _, h=h, rows=rows):
            cols = pl.ds(pl.multiple_of(i * WIDE, WIDE), WIDE)
            if h == 0:
                step1(i).wait_recv()
                it1[:, cols] = (i1p[:, cols] + i1r[:, cols]).astype(BF16)
            lhs = jnp.concatenate([it0[:, cols], it1[:, cols]], axis=0)
            up[:, rows] += dot_t(lhs, adj[rows, cols])
            return 0

        with jax.named_scope("ph_user"):
            lax.fori_loop(0, nst, user_step, 0)
        rc_up.append(remote(up.at[:, rows], up_r.at[:, rows], ssem.at[4 + h], rsem.at[4 + h], xpeer))
        rc_up[h].start()
    pl.semaphore_signal(free_sem, inc=1, device_id=sib, device_id_type=MESH)

    remote(i1p, i1r, cs1, cr1.at[0], sib).wait_send()

    def sel_step(g, _):
        users = lax.broadcasted_iota(jnp.int32, (16, 128), 0) + g * 16
        for t in range(nhome // 128):
            ids = tri_row(0, home_row(0) + t)
            hit = jnp.where(users == jnp.broadcast_to(ids, (16, 128)), 1.0, 0.0)
            sel[pl.ds(pl.multiple_of(g * 16, 16), 16), t * 128:(t + 1) * 128] = hit.astype(BF16)
        return 0

    with jax.named_scope("ph_sel"):
        lax.fori_loop(0, 2 * n_usr // 16, sel_step, 0, unroll=2)
    with jax.named_scope("ph_up_wait"):
        rc_up[0].wait()
        rc_up[1].wait()
    u12 = (up[...] + up_r[...]).astype(BF16)

    def part2(i, size, step):
        cols = pl.ds(pl.multiple_of(i * size, size), size)
        return remote(i2p.at[:, cols], i2r.at[:, cols], cs2, cr2.at[step], sib)

    def item_step(i, _):
        cols = pl.ds(pl.multiple_of(i * NARROW, NARROW), NARROW)
        part = jnp.dot(u12, adj[:, cols], preferred_element_type=F32)
        i2p[:, cols] = part[0:dim]
        i1p[:, cols] = part[dim:2 * dim]
        part2(i, NARROW, i // (WIDE // NARROW)).start()
        return 0

    with jax.named_scope("ph_item"):
        lax.fori_loop(0, n_itm // NARROW, item_step, 0)
        pl.semaphore_wait(free_sem, 1)
        for i in range(nst):
            step1(i).start()

    u3p[...] = jnp.zeros_like(u3p)

    def user3_step(i, _):
        cols = pl.ds(pl.multiple_of(i * WIDE, WIDE), WIDE)
        part2(i, WIDE, i).wait_recv()
        v2 = (i2p[:, cols] + i2r[:, cols]).astype(BF16)
        it2[:, cols] = v2
        u3p[...] += dot_t(adj[:, cols], v2).T
        return 0

    with jax.named_scope("ph_user3"):
        lax.fori_loop(0, nst, user3_step, 0)
    rc_u3 = remote(u3p, u3_r, ssem.at[6], rsem.at[6], xpeer)
    rc_u3.start()

    def final_step(k, _):
        cols = pl.ds(pl.multiple_of(k * FIN, FIN), FIN)
        v3 = (i1p[:, cols] + i1r[:, cols]).astype(BF16)
        acc = it0[:, cols].astype(F32) + it1[:, cols].astype(F32)
        acc = (acc + it2[:, cols].astype(F32)) + v3.astype(F32)
        fin = (acc * (1.0 / (NUM_LAYERS + 1))).astype(BF16)
        it1[:, cols] = fin
        fin = fin.astype(F32)
        for b in range(FIN // 128):
            table[pl.ds(pl.multiple_of(k * FIN + b * 128, 128), 128), :] = fin[:, b * 128:(b + 1) * 128].T
        return 0

    with jax.named_scope("ph_final"):
        for i in range(nst):
            step1(i).wait_recv()
        lax.fori_loop(0, n_itm // FIN, final_step, 0)
    oi_ref[...] = it1[:, pl.ds(pl.multiple_of(r * half, half), half)]

    def diff_rows(q, row0):
        def body(al, _):
            for row in (row0, row0 + 1):
                p = idx_s[al, q * nrow + row]
                n = idx_s[al, ncol + q * nrow + row]
                dbuf[pl.ds(row * 128 + al, 1), :] = table[pl.ds(p, 1), :] - table[pl.ds(n, 1), :]
            return 0

        lax.fori_loop(0, 128, body, 0, unroll=16)
        for row in (row0, row0 + 1):
            dt[q, :, row * 128:(row + 1) * 128] = dbuf[row * 128:(row + 1) * 128, :].T

    with jax.named_scope("ph_diff"):
        for row0 in range(0, nrow, 2):
            diff_rows(1, row0)
            cols = pl.ds(row0 * 128, 256)
            remote(dt.at[1, :, cols], drecv.at[:, cols], ds, dr, xpeer).start()

    with jax.named_scope("ph_u3_wait"):
        rc_u3.wait()
    u3 = (u3p[...] + u3_r[...]).astype(BF16).astype(F32)
    uacc = ut0[...].astype(F32) + u12[0:dim].astype(F32)
    uacc = (uacc + u12[dim:2 * dim].astype(F32)) + u3
    fin_u = (uacc * (1.0 / (NUM_LAYERS + 1))).astype(BF16)
    own_cols = pl.ds(pl.multiple_of(r * n_usr, n_usr), n_usr)
    uall[:, own_cols] = fin_u
    rc_uf = remote(uall.at[:, own_cols], uall.at[:, own_cols], ssem.at[7], rsem.at[7], sib)
    rc_uf.start()
    ou_ref[...] = uall[:, pl.ds(pl.multiple_of(r * n_usr + c * uh, uh), uh)]
    with jax.named_scope("ph_diff"):
        for row0 in range(0, nrow, 2):
            diff_rows(0, row0)
    with jax.named_scope("ph_uf_wait"):
        rc_uf.wait()
    urow = jnp.dot(uall[...], sel[...], preferred_element_type=F32)

    with jax.named_scope("ph_d_wait"):
        remote(dt.at[1], drecv, ds, dr, xpeer).wait()
    score = jnp.sum((dt[0] + drecv[...]) * urow, axis=0, keepdims=True)
    for row in range(nrow):
        sbuf[pl.ds(row, 1), :] = score[:, row * 128:(row + 1) * 128]

    def s_send(q):
        dev = {"emb": lax.rem(e + q // 4, 2), "col": lax.rem(c + (q // 2) % 2, 2), "row": lax.rem(r + q % 2, 2)}
        return remote(sbuf, srecv.at[q - 1], bs, br, dev)

    for q in range(7, 0, -1):
        s_send(q).start()
    with jax.named_scope("ph_s_wait"):
        remote(srecv, srecv, bs, br, sib).wait()
    for q in range(4):
        own = sbuf[...] if q == 0 else srecv[q - 1]
        x = own + srecv[q + 3]
        hq = lax.rem(c + q // 2, 2) * 2 + lax.rem(r + q % 2, 2)
        ls = jnp.maximum(-x, 0.0) + jnp.log1p(jnp.exp(-jnp.abs(x)))
        loss_ref[pl.ds(pl.multiple_of(hq * (nhome // 128), 8), nhome // 128), :] = ls

    with jax.named_scope("ph_drain"):
        remote(i2p, i2r, cs2, cr2.at[0], sib).wait_send()
        remote(i1p, i1r, cs1, cr1.at[0], sib).wait_send()


def store_kernel(*refs):
    srcs, dsts, sem = refs[0:3], refs[3:6], refs[6]
    copies = [pltpu.make_async_copy(a, b, sem.at[k]) for k, (a, b) in enumerate(zip(srcs, dsts))]
    for copy in copies:
        copy.start()
    for copy in copies:
        copy.wait()


def solution(mesh):
    def local_fn(mask_blk, user_sh, item_sh, triples):
        n_usr, n_itm = mask_blk.shape
        dim = user_sh.shape[1]
        n_trip = triples.shape[0]
        nch = n_itm // CH
        half = n_itm // 2
        tri = triples.T
        vm = pltpu.VMEM
        dma = pltpu.SemaphoreType.DMA
        nhome = n_trip // 4
        hrow = nhome // 4
        scratch = [
            vm((NSLOT, n_usr, MC), jnp.int32), vm((n_usr, n_itm + 128), BF16), vm((n_usr, 128), F32),
            vm((n_itm // MC, MC), F32), vm((n_itm // MC, MC), F32), vm((1, n_usr), F32), vm((1, n_usr), F32),
            vm((n_usr, 128), F32), vm((n_itm // MC, MC), F32),
            vm((dim, n_itm), BF16), vm((dim, n_itm), BF16), vm((dim, n_itm), BF16), vm((dim, n_usr), BF16),
            vm((dim, n_itm), F32), vm((dim, n_itm), F32), vm((dim, n_itm), F32), vm((dim, n_itm), F32),
            vm((2 * dim, n_usr), F32), vm((2 * dim, n_usr), F32), vm((dim, n_usr), F32), vm((dim, n_usr), F32),
            vm((dim, 2 * n_usr), BF16), vm((2 * n_usr, nhome), BF16),
            vm((n_itm + 8, dim), F32),
            vm((3, n_trip), jnp.int32), vm((128, 128), jnp.int32), vm((128, 128), jnp.int32),
            pltpu.SMEM((128, 128), jnp.int32),
            vm((nhome, dim), F32), vm((2, dim, nhome), F32), vm((dim, nhome), F32),
            vm((nhome // 128, 128), F32), vm((7, nhome // 128, 128), F32),
            dma((NSLOT,)), dma((3,)), dma((8,)), dma((8,)),
            dma(()), dma((n_itm // WIDE,)), dma(()), dma((n_itm // WIDE,)),
            dma(()), dma(()), dma(()), dma(()), pltpu.SemaphoreType.REGULAR,
        ]
        hbm_spec = pl.BlockSpec(memory_space=pltpu.HBM)
        vmem_spec = pl.BlockSpec(memory_space=pltpu.VMEM)
        ou, oi, loss = pl.pallas_call(
            functools.partial(kernel, n_usr, n_itm, dim, n_trip),
            out_shape=(jax.ShapeDtypeStruct((dim, n_usr // 2), BF16),
                       jax.ShapeDtypeStruct((dim, half), BF16),
                       jax.ShapeDtypeStruct((n_trip // 128, 128), F32)),
            in_specs=[hbm_spec] * 4,
            out_specs=(vmem_spec,) * 3,
            scratch_shapes=scratch,
            compiler_params=pltpu.CompilerParams(collective_id=0, has_side_effects=True,
                                                 vmem_limit_bytes=50 * 1024 * 1024),
            name="gcn",
        )(mask_blk, *[pltpu.with_memory_space_constraint(v, pltpu.HBM) for v in (user_sh.T, item_sh.T, tri)])
        ou, oi, loss = pl.pallas_call(
            store_kernel,
            out_shape=tuple(jax.ShapeDtypeStruct(v.shape, v.dtype) for v in (ou, oi, loss)),
            in_specs=[vmem_spec] * 3,
            out_specs=(pl.BlockSpec(memory_space=pl.ANY),) * 3,
            scratch_shapes=[dma((3,))],
            compiler_params=pltpu.CompilerParams(vmem_limit_bytes=4 * 1024 * 1024),
            name="store",
        )(ou, oi, loss)
        return ou.T, oi.T, loss.reshape(n_trip)

    return jax.shard_map(
        local_fn, mesh=mesh,
        in_specs=(P("row", "col"), P(("row", "col"), "emb"), P(("col", "row"), "emb"), P()),
        out_specs=(P(("row", "col"), "emb"), P(("col", "row"), "emb"), P()),
        check_vma=False)
```

time: 55.5 us -> 50.9 us (0.917)
  Pallas kernels: 54.8 us -> 50.1 us
    pallas_call x1, Pallas kernels: 53.9 us -> 49.3 us  [local_fn(): pl.pallas_call(functools.partial(kernel, n_usr, n_itm, dim, n_trip), out_...]
where the time goes in v4:
time: 50.9 us; the launch traced here: 50.8 us
  Pallas kernels  50.1 us (98%)
  between operations  0.64 us (1%)
    pallas_call x1, Pallas kernels, local_fn(): pl.pallas_call(functools.partial(kernel, n_usr, n_itm, dim, n_trip), out_...  49.3 us

profile of v4, /device:TPU:0, one launch (start us, length us, event | category | flops | bytes accessed | tf_op | source)
XLA Modules:
  0.0 50.8 jit_solution(940187135084049699)
XLA Ops:
  0.6 49.3 %gcn.1 = (bf16[32,256]{1,0:T(8,128)(2,1)S(1)}, bf16[32,8192]{1,0:T(8,128)(2,1)S(1)}, f32[32,128]{1,0:T(8,128)S(1)}) custom-call(s32[512,16384]{1,0:T(8,128)} %mask_ref.1, bf16[32,256]{1,0:T(8,128)(2,1)} %bitcast.8, bf16[32,8192]{1,0:T(8,128)(2,1)} %bitcast.6, s32[3,4096]{1,0:T(4,128)} %bitcast.7), custom_call_target="tpu_custom_call" | custom-call | tf_op jit(solution)/shard_map/gcn/pallas_call | solution.py:368
  50.0 0.8 %store.1 = (bf16[32,256]{1,0:T(8,128)(2,1)}, bf16[32,8192]{1,0:T(8,128)(2,1)}, f32[32,128]{1,0:T(8,128)}) custom-call(bf16[32,256]{1,0:T(8,128)(2,1)S(1)} %get-tuple-element.9.refs_0_, bf16[32,8192]{1,0:T(8,128)(2,1)S(1)} %get-tuple-element.10.refs_1_, f32[32,128]{1,0:T(8,128)S(1)} %get-tuple-element.11.refs_2_), custom_call_target="tpu_custom_call" | custom-call | tf_op jit(solution)/shard_map/store/pallas_call | solution.py:380

commit v5 on v4

--- a/solution.py
+++ b/solution.py
@@ -175,10 +175,21 @@
     def dot_t(a, b):
         return lax.dot_general(a, b, (((1,), (1,)), ((), ())), preferred_element_type=F32)
 
+    def mixed_t(vals, rows, i):
+        acc1 = acc2 = None
+        for lo in range(0, WIDE, 512):
+            ca = pl.ds(pl.multiple_of(i * WIDE + lo, 256), 256)
+            cb = pl.ds(pl.multiple_of(i * WIDE + lo + 256, 256), 256)
+            p1 = dot_t(vals[:, lo:lo + 256], adj[rows, ca])
+            p2 = dot_t(adj[rows, cb], vals[:, lo + 256:lo + 512])
+            acc1 = p1 if acc1 is None else acc1 + p1
+            acc2 = p2 if acc2 is None else acc2 + p2
+        return acc1 + acc2.T
+
     up[...] = jnp.zeros_like(up)
     rc_up = []
-    for h in range(2):
-        rows = pl.ds(h * uh, uh)
+    for h in range(1):
+        rows = pl.ds(0, n_usr)
 
         def user_step(i, _, h=h, rows=rows):
             cols = pl.ds(pl.multiple_of(i * WIDE, WIDE), WIDE)
@@ -186,7 +197,7 @@
                 step1(i).wait_recv()
                 it1[:, cols] = (i1p[:, cols] + i1r[:, cols]).astype(BF16)
             lhs = jnp.concatenate([it0[:, cols], it1[:, cols]], axis=0)
-            up[:, rows] += dot_t(lhs, adj[rows, cols])
+            up[:, rows] += mixed_t(lhs, rows, i)
             return 0
 
         with jax.named_scope("ph_user"):
@@ -209,7 +220,6 @@
         lax.fori_loop(0, 2 * n_usr // 16, sel_step, 0, unroll=2)
     with jax.named_scope("ph_up_wait"):
         rc_up[0].wait()
-        rc_up[1].wait()
     u12 = (up[...] + up_r[...]).astype(BF16)
 
     def part2(i, size, step):
@@ -237,7 +247,7 @@
         part2(i, WIDE, i).wait_recv()
         v2 = (i2p[:, cols] + i2r[:, cols]).astype(BF16)
         it2[:, cols] = v2
-        u3p[...] += dot_t(adj[:, cols], v2).T
+        u3p[...] += mixed_t(v2, slice(None), i)
         return 0
 
     with jax.named_scope("ph_user3"):
@@ -347,7 +357,7 @@
         nhome = n_trip // 4
         hrow = nhome // 4
         scratch = [
-            vm((NSLOT, n_usr, MC), jnp.int32), vm((n_usr, n_itm + 128), BF16), vm((n_usr, 128), F32),
+            vm((NSLOT, n_usr, MC), jnp.int32), vm((n_usr, n_itm + 256), BF16), vm((n_usr, 128), F32),
             vm((n_itm // MC, MC), F32), vm((n_itm // MC, MC), F32), vm((1, n_usr), F32), vm((1, n_usr), F32),
             vm((n_usr, 128), F32), vm((n_itm // MC, MC), F32),
             vm((dim, n_itm), BF16), vm((dim, n_itm), BF16), vm((dim, n_itm), BF16), vm((dim, n_usr), BF16),

time: 50.9 us -> 48.9 us (0.961)
  Pallas kernels: 50.1 us -> 48.2 us
    pallas_call x1, Pallas kernels: 49.3 us -> 47.4 us  [local_fn(): pl.pallas_call(functools.partial(kernel, n_usr, n_itm, dim, n_trip), out_...]
where the time goes in v5:
time: 48.9 us; the launch traced here: 48.8 us
  Pallas kernels  48.2 us (99%)
  between operations  0.64 us (1%)
    pallas_call x1, Pallas kernels, local_fn(): pl.pallas_call(functools.partial(kernel, n_usr, n_itm, dim, n_trip), out_...  47.4 us

profile of v5, /device:TPU:0, one launch (start us, length us, event | category | flops | bytes accessed | tf_op | source)
XLA Modules:
  0.0 48.8 jit_solution(16261434906007704095)
XLA Ops:
  0.6 47.4 %gcn.1 = (bf16[32,256]{1,0:T(8,128)(2,1)S(1)}, bf16[32,8192]{1,0:T(8,128)(2,1)S(1)}, f32[32,128]{1,0:T(8,128)S(1)}) custom-call(s32[512,16384]{1,0:T(8,128)} %mask_ref.1, bf16[32,256]{1,0:T(8,128)(2,1)} %bitcast.8, bf16[32,8192]{1,0:T(8,128)(2,1)} %bitcast.6, s32[3,4096]{1,0:T(4,128)} %bitcast.7), custom_call_target="tpu_custom_call" | custom-call | tf_op jit(solution)/shard_map/gcn/pallas_call | solution.py:378
  48.0 0.8 %store.1 = (bf16[32,256]{1,0:T(8,128)(2,1)}, bf16[32,8192]{1,0:T(8,128)(2,1)}, f32[32,128]{1,0:T(8,128)}) custom-call(bf16[32,256]{1,0:T(8,128)(2,1)S(1)} %get-tuple-element.9.refs_0_, bf16[32,8192]{1,0:T(8,128)(2,1)S(1)} %get-tuple-element.10.refs_1_, f32[32,128]{1,0:T(8,128)S(1)} %get-tuple-element.11.refs_2_), custom_call_target="tpu_custom_call" | custom-call | tf_op jit(solution)/shard_map/store/pallas_call | solution.py:390

commit v6 on v5

--- a/solution.py
+++ b/solution.py
@@ -8,11 +8,13 @@
 from jax.sharding import PartitionSpec as P
 
 NUM_LAYERS = 3
+BIG = 4096
 CH = 2048
 MC = 512
-NSLOT = 6
+NSLOT = 8
 FIN = 4096
 WIDE = 8192
+FIRST = 2048
 NARROW = 4096
 MESH = pl.DeviceIdType.MESH
 F32 = jnp.float32
@@ -128,82 +130,76 @@
     table[pl.ds(n_itm, 8), :] = jnp.zeros((8, dim), F32)
 
     with jax.named_scope("ph_di_wait"):
-        rc_di.wait()
+        rc_di.wait_recv()
     invi[...] = lax.rsqrt(jnp.maximum(degi[...] + degi_r[...], 1.0))
-    rc_i.wait()
-    rc_u.wait()
+    rc_i.wait_recv()
+    rc_u.wait_recv()
     cp_x.wait()
     with jax.named_scope("ph_du_wait"):
-        rc_du.wait()
+        rc_du.wait_recv()
     inv_row = lax.rsqrt(jnp.maximum(degu[...] + degu_r[...], 1.0))
     invu[...] = jnp.broadcast_to(inv_row, (128, n_usr)).T
 
     nst = n_itm // WIDE
 
-    def chunk1(j):
-        cols = pl.ds(pl.multiple_of(j * CH, CH), CH)
-        return remote(i1p.at[:, cols], i1r.at[:, cols], cs1, cr1.at[j // (WIDE // CH)], sib)
+    def chunk1(base, size):
+        cols = pl.ds(pl.multiple_of(base, size), size)
+        return remote(i1p.at[:, cols], i1r.at[:, cols], cs1, cr1.at[base // WIDE], sib)
 
     def step1(i):
         cols = pl.ds(pl.multiple_of(i * WIDE, WIDE), WIDE)
         return remote(i1p.at[:, cols], i1r.at[:, cols], cs1, cr1.at[i], sib)
 
-    def build_step(j, _):
-        for nt in range(CH // 256):
-            cols = pl.ds(pl.multiple_of(j * CH + nt * 256, 256), 256)
+    def build_step(base, size):
+        for nt in range(size // 256):
+            cols = pl.ds(pl.multiple_of(base + nt * 256, 256), 256)
             lane = nt * 256 % MC
-            wi = jnp.broadcast_to(invi[pl.ds(j * (CH // MC) + nt * 256 // MC, 1), lane:lane + 256], (16, 256))
-            part = None
-            for kt in range(n_usr // 256):
-                tiles = []
-                for g in range(16):
-                    rows = pl.ds(kt * 256 + g * 16, 16)
-                    wu = jnp.concatenate([invu[rows, :]] * 2, axis=1)
-                    a = (wu * wi).astype(BF16) * adj[rows, cols]
-                    adj[rows, cols] = a
-                    tiles.append(a)
-                p = jnp.dot(ut0[:, kt * 256:(kt + 1) * 256], jnp.concatenate(tiles, axis=0),
-                            preferred_element_type=F32)
-                part = p if part is None else part + p
+            wi = jnp.broadcast_to(invi[pl.ds(base // MC + nt * 256 // MC, 1), lane:lane + 256], (16, 256))
+            tiles = []
+            for g in range(n_usr // 16):
+                rows = pl.ds(g * 16, 16)
+                wu = jnp.concatenate([invu[rows, :]] * 2, axis=1)
+                a = (wu * wi).astype(BF16) * adj[rows, cols]
+                adj[rows, cols] = a
+                tiles.append(a)
+            part = jnp.dot(ut0[...], jnp.concatenate(tiles, axis=0), preferred_element_type=F32)
             i1p[:, cols] = part
-        chunk1(j).start()
+        chunk1(base, size).start()
         return 0
 
     with jax.named_scope("ph_build"):
-        lax.fori_loop(0, nch, build_step, 0)
+        nbig = n_itm // BIG - 1
+        lax.fori_loop(0, nbig, lambda i, _: build_step(i * BIG, BIG), 0)
+        lax.fori_loop(0, BIG // CH, lambda i, _: build_step(nbig * BIG + i * CH, CH), 0)
 
     def dot_t(a, b):
         return lax.dot_general(a, b, (((1,), (1,)), ((), ())), preferred_element_type=F32)
 
-    def mixed_t(vals, rows, i):
+    def mixed_t(vals, base):
         acc1 = acc2 = None
         for lo in range(0, WIDE, 512):
-            ca = pl.ds(pl.multiple_of(i * WIDE + lo, 256), 256)
-            cb = pl.ds(pl.multiple_of(i * WIDE + lo + 256, 256), 256)
-            p1 = dot_t(vals[:, lo:lo + 256], adj[rows, ca])
-            p2 = dot_t(adj[rows, cb], vals[:, lo + 256:lo + 512])
+            ca = pl.ds(pl.multiple_of(base + lo, 256), 256)
+            cb = pl.ds(pl.multiple_of(base + lo + 256, 256), 256)
+            p1 = dot_t(vals[:, lo:lo + 256], adj[:, ca])
+            p2 = dot_t(adj[:, cb], vals[:, lo + 256:lo + 512])
             acc1 = p1 if acc1 is None else acc1 + p1
             acc2 = p2 if acc2 is None else acc2 + p2
         return acc1 + acc2.T
 
     up[...] = jnp.zeros_like(up)
-    rc_up = []
-    for h in range(1):
-        rows = pl.ds(0, n_usr)
-
-        def user_step(i, _, h=h, rows=rows):
-            cols = pl.ds(pl.multiple_of(i * WIDE, WIDE), WIDE)
-            if h == 0:
-                step1(i).wait_recv()
-                it1[:, cols] = (i1p[:, cols] + i1r[:, cols]).astype(BF16)
-            lhs = jnp.concatenate([it0[:, cols], it1[:, cols]], axis=0)
-            up[:, rows] += mixed_t(lhs, rows, i)
-            return 0
-
-        with jax.named_scope("ph_user"):
-            lax.fori_loop(0, nst, user_step, 0)
-        rc_up.append(remote(up.at[:, rows], up_r.at[:, rows], ssem.at[4 + h], rsem.at[4 + h], xpeer))
-        rc_up[h].start()
+
+    def user_step(i, _):
+        cols = pl.ds(pl.multiple_of(i * WIDE, WIDE), WIDE)
+        step1(i).wait_recv()
+        v1 = (i1p[:, cols] + i1r[:, cols]).astype(BF16)
+        it1[:, cols] = v1
+        up[...] += mixed_t(jnp.concatenate([it0[:, cols], v1], axis=0), i * WIDE)
+        return 0
+
+    with jax.named_scope("ph_user"):
+        lax.fori_loop(0, nst, user_step, 0)
+    rc_up = remote(up, up_r, ssem.at[4], rsem.at[4], xpeer)
+    rc_up.start()
     pl.semaphore_signal(free_sem, inc=1, device_id=sib, device_id_type=MESH)
 
     remote(i1p, i1r, cs1, cr1.at[0], sib).wait_send()
@@ -219,59 +215,85 @@
     with jax.named_scope("ph_sel"):
         lax.fori_loop(0, 2 * n_usr // 16, sel_step, 0, unroll=2)
     with jax.named_scope("ph_up_wait"):
-        rc_up[0].wait()
+        rc_up.wait_recv()
     u12 = (up[...] + up_r[...]).astype(BF16)
 
-    def part2(i, size, step):
-        cols = pl.ds(pl.multiple_of(i * size, size), size)
-        return remote(i2p.at[:, cols], i2r.at[:, cols], cs2, cr2.at[step], sib)
-
-    def item_step(i, _):
-        cols = pl.ds(pl.multiple_of(i * NARROW, NARROW), NARROW)
+    oo = r * half
+    so = (1 - r) * half
+    own = pl.ds(pl.multiple_of(oo, half), half)
+    other = pl.ds(pl.multiple_of(so, half), half)
+
+    def half2(k, size):
+        src = pl.ds(pl.multiple_of(so + k * size, size), size)
+        dst = pl.ds(pl.multiple_of(k * size, size), size)
+        return remote(i2p.at[:, src], i2r.at[:, dst], cs2, cr2, sib)
+
+    def half3(cols):
+        return remote(i1p.at[:, cols], i1r.at[:, cols], cs1, cr1.at[0], sib)
+
+    def rounded(ref, cols, k):
+        return remote(ref.at[:, cols], ref.at[:, cols], ssem.at[k], rsem.at[k], sib)
+
+    def item_step(k, base, size, send):
+        cols = pl.ds(pl.multiple_of(base + k * size, size), size)
         part = jnp.dot(u12, adj[:, cols], preferred_element_type=F32)
         i2p[:, cols] = part[0:dim]
         i1p[:, cols] = part[dim:2 * dim]
-        part2(i, NARROW, i // (WIDE // NARROW)).start()
-        return 0
+        if send:
+            half2(k, size).start()
 
     with jax.named_scope("ph_item"):
-        lax.fori_loop(0, n_itm // NARROW, item_step, 0)
+        for k in range(half // FIRST):
+            item_step(k, so, FIRST, True)
         pl.semaphore_wait(free_sem, 1)
-        for i in range(nst):
-            step1(i).start()
-
-    u3p[...] = jnp.zeros_like(u3p)
-
-    def user3_step(i, _):
-        cols = pl.ds(pl.multiple_of(i * WIDE, WIDE), WIDE)
-        part2(i, WIDE, i).wait_recv()
-        v2 = (i2p[:, cols] + i2r[:, cols]).astype(BF16)
-        it2[:, cols] = v2
-        u3p[...] += mixed_t(v2, slice(None), i)
-        return 0
-
+        half3(other).start()
+        for k in range(half // NARROW):
+            item_step(k, oo, NARROW, False)
+    with jax.named_scope("ph_i2_wait"):
+        half2(0, half).wait_recv()
+    it2[:, own] = (i2p[:, own] + i2r[...]).astype(BF16)
+    rounded(it2, own, 5).start()
     with jax.named_scope("ph_user3"):
-        lax.fori_loop(0, nst, user3_step, 0)
-    rc_u3 = remote(u3p, u3_r, ssem.at[6], rsem.at[6], xpeer)
-    rc_u3.start()
+        u3p[...] = mixed_t(it2[:, own], oo)
+
+    def table_step(fin, base):
+        fin = fin.astype(F32)
+        for b in range(FIN // 128):
+            table[pl.ds(pl.multiple_of(base + b * 128, 128), 128), :] = fin[:, b * 128:(b + 1) * 128].T
 
     def final_step(k, _):
-        cols = pl.ds(pl.multiple_of(k * FIN, FIN), FIN)
+        base = oo + k * FIN
+        cols = pl.ds(pl.multiple_of(base, FIN), FIN)
         v3 = (i1p[:, cols] + i1r[:, cols]).astype(BF16)
         acc = it0[:, cols].astype(F32) + it1[:, cols].astype(F32)
         acc = (acc + it2[:, cols].astype(F32)) + v3.astype(F32)
         fin = (acc * (1.0 / (NUM_LAYERS + 1))).astype(BF16)
         it1[:, cols] = fin
-        fin = fin.astype(F32)
-        for b in range(FIN // 128):
-            table[pl.ds(pl.multiple_of(k * FIN + b * 128, 128), 128), :] = fin[:, b * 128:(b + 1) * 128].T
-        return 0
-
+        rounded(it1, cols, 8).start()
+        table_step(fin, base)
+        return 0
+
+    with jax.named_scope("ph_i3_wait"):
+        half3(own).wait_recv()
     with jax.named_scope("ph_final"):
-        for i in range(nst):
-            step1(i).wait_recv()
-        lax.fori_loop(0, n_itm // FIN, final_step, 0)
-    oi_ref[...] = it1[:, pl.ds(pl.multiple_of(r * half, half), half)]
+        lax.fori_loop(0, half // FIN, final_step, 0)
+    oi_ref[...] = it1[:, own]
+    with jax.named_scope("ph_i2b_wait"):
+        rounded(it2, other, 5).wait_recv()
+    with jax.named_scope("ph_user3"):
+        u3p[...] += mixed_t(it2[:, other], so)
+    rc_u3 = remote(u3p, u3_r, ssem.at[6], rsem.at[6], xpeer)
+    rc_u3.start()
+
+    def other_step(k, _):
+        base = so + k * FIN
+        table_step(it1[:, pl.ds(pl.multiple_of(base, FIN), FIN)], base)
+        return 0
+
+    with jax.named_scope("ph_i3b_wait"):
+        rounded(it1, other, 8).wait_recv()
+    with jax.named_scope("ph_final"):
+        lax.fori_loop(0, half // FIN, other_step, 0)
 
     def diff_rows(q, row0):
         def body(al, _):
@@ -291,8 +313,12 @@
             cols = pl.ds(row0 * 128, 256)
             remote(dt.at[1, :, cols], drecv.at[:, cols], ds, dr, xpeer).start()
 
+    with jax.named_scope("ph_diff"):
+        for row0 in range(0, nrow // 2, 2):
+            diff_rows(0, row0)
+
     with jax.named_scope("ph_u3_wait"):
-        rc_u3.wait()
+        rc_u3.wait_recv()
     u3 = (u3p[...] + u3_r[...]).astype(BF16).astype(F32)
     uacc = ut0[...].astype(F32) + u12[0:dim].astype(F32)
     uacc = (uacc + u12[dim:2 * dim].astype(F32)) + u3
@@ -303,14 +329,14 @@
     rc_uf.start()
     ou_ref[...] = uall[:, pl.ds(pl.multiple_of(r * n_usr + c * uh, uh), uh)]
     with jax.named_scope("ph_diff"):
-        for row0 in range(0, nrow, 2):
+        for row0 in range(nrow // 2, nrow, 2):
             diff_rows(0, row0)
     with jax.named_scope("ph_uf_wait"):
-        rc_uf.wait()
+        rc_uf.wait_recv()
     urow = jnp.dot(uall[...], sel[...], preferred_element_type=F32)
 
     with jax.named_scope("ph_d_wait"):
-        remote(dt.at[1], drecv, ds, dr, xpeer).wait()
+        remote(dt.at[1], drecv, ds, dr, xpeer).wait_recv()
     score = jnp.sum((dt[0] + drecv[...]) * urow, axis=0, keepdims=True)
     for row in range(nrow):
         sbuf[pl.ds(row, 1), :] = score[:, row * 128:(row + 1) * 128]
@@ -322,17 +348,22 @@
     for q in range(7, 0, -1):
         s_send(q).start()
     with jax.named_scope("ph_s_wait"):
-        remote(srecv, srecv, bs, br, sib).wait()
+        remote(srecv, srecv, bs, br, sib).wait_recv()
     for q in range(4):
-        own = sbuf[...] if q == 0 else srecv[q - 1]
-        x = own + srecv[q + 3]
+        mine = sbuf[...] if q == 0 else srecv[q - 1]
+        x = mine + srecv[q + 3]
         hq = lax.rem(c + q // 2, 2) * 2 + lax.rem(r + q % 2, 2)
         ls = jnp.maximum(-x, 0.0) + jnp.log1p(jnp.exp(-jnp.abs(x)))
         loss_ref[pl.ds(pl.multiple_of(hq * (nhome // 128), 8), nhome // 128), :] = ls
 
     with jax.named_scope("ph_drain"):
-        remote(i2p, i2r, cs2, cr2.at[0], sib).wait_send()
-        remote(i1p, i1r, cs1, cr1.at[0], sib).wait_send()
+        half2(0, half).wait_send()
+        half3(other).wait_send()
+        rounded(it2, own, 5).wait_send()
+        rounded(it1, own, 8).wait_send()
+        for copy in (rc_i, rc_u, rc_du, rc_di, rc_up, rc_u3, rc_uf, remote(dt.at[1], drecv, ds, dr, xpeer),
+                     remote(srecv, srecv, bs, br, sib)):
+            copy.wait_send()
 
 
 def store_kernel(*refs):
@@ -361,7 +392,7 @@
             vm((n_itm // MC, MC), F32), vm((n_itm // MC, MC), F32), vm((1, n_usr), F32), vm((1, n_usr), F32),
             vm((n_usr, 128), F32), vm((n_itm // MC, MC), F32),
             vm((dim, n_itm), BF16), vm((dim, n_itm), BF16), vm((dim, n_itm), BF16), vm((dim, n_usr), BF16),
-            vm((dim, n_itm), F32), vm((dim, n_itm), F32), vm((dim, n_itm), F32), vm((dim, n_itm), F32),
+            vm((dim, n_itm), F32), vm((dim, n_itm), F32), vm((dim, n_itm), F32), vm((dim, half), F32),
             vm((2 * dim, n_usr), F32), vm((2 * dim, n_usr), F32), vm((dim, n_usr), F32), vm((dim, n_usr), F32),
             vm((dim, 2 * n_usr), BF16), vm((2 * n_usr, nhome), BF16),
             vm((n_itm + 8, dim), F32),
@@ -369,8 +400,8 @@
             pltpu.SMEM((128, 128), jnp.int32),
             vm((nhome, dim), F32), vm((2, dim, nhome), F32), vm((dim, nhome), F32),
             vm((nhome // 128, 128), F32), vm((7, nhome // 128, 128), F32),
-            dma((NSLOT,)), dma((3,)), dma((8,)), dma((8,)),
-            dma(()), dma((n_itm // WIDE,)), dma(()), dma((n_itm // WIDE,)),
+            dma((NSLOT,)), dma((3,)), dma((9,)), dma((9,)),
+            dma(()), dma((n_itm // WIDE,)), dma(()), dma(()),
             dma(()), dma(()), dma(()), dma(()), pltpu.SemaphoreType.REGULAR,
         ]
         hbm_spec = pl.BlockSpec(memory_space=pltpu.HBM)

time: 48.9 us -> 47.8 us (0.978)
  Pallas kernels: 48.2 us -> 47.1 us
    pallas_call x1, Pallas kernels: 47.4 us -> 46.3 us  [local_fn(): pl.pallas_call(functools.partial(kernel, n_usr, n_itm, dim, n_trip), out_...]
where the time goes in v6:
time: 47.8 us; the launch traced here: 47.7 us
  Pallas kernels  47.1 us (99%)
  between operations  0.64 us (1%)
    pallas_call x1, Pallas kernels, local_fn(): pl.pallas_call(functools.partial(kernel, n_usr, n_itm, dim, n_trip), out_...  46.3 us

profile of v6, /device:TPU:0, one launch (start us, length us, event | category | flops | bytes accessed | tf_op | source)
XLA Modules:
  0.0 47.7 jit_solution(8859583296696266063)
XLA Ops:
  0.6 46.3 %gcn.1 = (bf16[32,256]{1,0:T(8,128)(2,1)S(1)}, bf16[32,8192]{1,0:T(8,128)(2,1)S(1)}, f32[32,128]{1,0:T(8,128)S(1)}) custom-call(s32[512,16384]{1,0:T(8,128)} %mask_ref.1, bf16[32,256]{1,0:T(8,128)(2,1)} %bitcast.8, bf16[32,8192]{1,0:T(8,128)(2,1)} %bitcast.6, s32[3,4096]{1,0:T(4,128)} %bitcast.7), custom_call_target="tpu_custom_call" | custom-call | tf_op jit(solution)/shard_map/gcn/pallas_call | solution.py:409
  46.9 0.8 %store.1 = (bf16[32,256]{1,0:T(8,128)(2,1)}, bf16[32,8192]{1,0:T(8,128)(2,1)}, f32[32,128]{1,0:T(8,128)}) custom-call(bf16[32,256]{1,0:T(8,128)(2,1)S(1)} %get-tuple-element.9.refs_0_, bf16[32,8192]{1,0:T(8,128)(2,1)S(1)} %get-tuple-element.10.refs_1_, f32[32,128]{1,0:T(8,128)S(1)} %get-tuple-element.11.refs_2_), custom_call_target="tpu_custom_call" | custom-call | tf_op jit(solution)/shard_map/store/pallas_call | solution.py:421

commit v7 on v6

--- a/solution.py
+++ b/solution.py
@@ -31,8 +31,9 @@
            stage, adj, rowacc, degi, degi_r, degu, degu_r, invu, invi,
            it0, it1, it2, ut0, i1p, i1r, i2p, i2r,
            up, up_r, u3p, u3_r, uall, sel, table,
-           tri_v, idx_v, idx_t, idx_s, dbuf, dt, drecv, sbuf, srecv,
-           msem, lsem, ssem, rsem, cs1, cr1, cs2, cr2, ds, dr, bs, br, free_sem):
+           tri_v, idx_v, s0, s1, s2, s3, s4, s5, s6, s7, dbuf, dt, drecv, sbuf, srecv,
+           msem, lsem, ssem, rsem, cs1, cr1, cs2, cr2, ds, dr, bs, br, xsem, free_sem):
+    idx_s = (s0, s1, s2, s3, s4, s5, s6, s7)
     e = lax.axis_index("emb")
     c = lax.axis_index("col")
     r = lax.axis_index("row")
@@ -116,17 +117,18 @@
         return (lax.rem(c + q, 2) * 2 + r) * (nhome // 128)
 
     nrow = nhome // 128
-    ncol = 2 * nrow
     idx_v[...] = jnp.zeros_like(idx_v)
     for k in range(2):
         for q in range(2):
             for row in range(nrow):
-                idx_v[pl.ds(k * ncol + q * nrow + row, 1), :] = tri_row(k + 1, home_row(q) + row)
-    loc = idx_v[0:2 * ncol, :] - c * n_itm
-    idx_v[0:2 * ncol, :] = jnp.where((loc >= 0) & (loc < n_itm), loc, n_itm)
-    idx_t[...] = idx_v[...].T
-    cp_x = pltpu.make_async_copy(idx_t, idx_s, lsem.at[0])
-    cp_x.start()
+                loc = tri_row(k + 1, home_row(q) + row) - c * n_itm
+                loc = jnp.where((loc >= 0) & (loc < n_itm), loc, n_itm)
+                for t in range(4):
+                    idx_v[k * 4 + t, :, pl.ds((q * nrow + row) * 128, 32)] = loc[:, t * 32:(t + 1) * 32]
+    cp_x = []
+    for t in range(8):
+        cp_x.append(pltpu.make_async_copy(idx_v.at[t], idx_s[t], xsem.at[t]))
+        cp_x[t].start()
     table[pl.ds(n_itm, 8), :] = jnp.zeros((8, dim), F32)
 
     with jax.named_scope("ph_di_wait"):
@@ -134,7 +136,8 @@
     invi[...] = lax.rsqrt(jnp.maximum(degi[...] + degi_r[...], 1.0))
     rc_i.wait_recv()
     rc_u.wait_recv()
-    cp_x.wait()
+    for t in range(8):
+        cp_x[t].wait()
     with jax.named_scope("ph_du_wait"):
         rc_du.wait_recv()
     inv_row = lax.rsqrt(jnp.maximum(degu[...] + degu_r[...], 1.0))
@@ -175,7 +178,7 @@
     def dot_t(a, b):
         return lax.dot_general(a, b, (((1,), (1,)), ((), ())), preferred_element_type=F32)
 
-    def mixed_t(vals, base):
+    def mixed_t(vals, base, beside=None):
         acc1 = acc2 = None
         for lo in range(0, WIDE, 512):
             ca = pl.ds(pl.multiple_of(base + lo, 256), 256)
@@ -184,6 +187,8 @@
             p2 = dot_t(adj[:, cb], vals[:, lo + 256:lo + 512])
             acc1 = p1 if acc1 is None else acc1 + p1
             acc2 = p2 if acc2 is None else acc2 + p2
+            if beside:
+                beside(lo)
         return acc1 + acc2.T
 
     up[...] = jnp.zeros_like(up)
@@ -270,7 +275,6 @@
         fin = (acc * (1.0 / (NUM_LAYERS + 1))).astype(BF16)
         it1[:, cols] = fin
         rounded(it1, cols, 8).start()
-        table_step(fin, base)
         return 0
 
     with jax.named_scope("ph_i3_wait"):
@@ -278,44 +282,52 @@
     with jax.named_scope("ph_final"):
         lax.fori_loop(0, half // FIN, final_step, 0)
     oi_ref[...] = it1[:, own]
+
+    def own_rows(lo):
+        for b in range(4):
+            at = pl.ds(pl.multiple_of(oo + lo + b * 128, 128), 128)
+            table[at, :] = it1[:, at].astype(F32).T
+
     with jax.named_scope("ph_i2b_wait"):
         rounded(it2, other, 5).wait_recv()
     with jax.named_scope("ph_user3"):
-        u3p[...] += mixed_t(it2[:, other], so)
+        u3p[...] += mixed_t(it2[:, other], so, own_rows)
     rc_u3 = remote(u3p, u3_r, ssem.at[6], rsem.at[6], xpeer)
     rc_u3.start()
 
-    def other_step(k, _):
-        base = so + k * FIN
+    def rows_step(k, start):
+        base = start + k * FIN
         table_step(it1[:, pl.ds(pl.multiple_of(base, FIN), FIN)], base)
         return 0
+
 
     with jax.named_scope("ph_i3b_wait"):
         rounded(it1, other, 8).wait_recv()
     with jax.named_scope("ph_final"):
-        lax.fori_loop(0, half // FIN, other_step, 0)
-
-    def diff_rows(q, row0):
-        def body(al, _):
-            for row in (row0, row0 + 1):
-                p = idx_s[al, q * nrow + row]
-                n = idx_s[al, ncol + q * nrow + row]
-                dbuf[pl.ds(row * 128 + al, 1), :] = table[pl.ds(p, 1), :] - table[pl.ds(n, 1), :]
+        lax.fori_loop(0, half // FIN, lambda k, _: rows_step(k, so), 0)
+
+    def diff_row(q, row):
+        def body(i, _):
+            for u in range(8):
+                at = (q * nrow + row) * 128 + i * 8 + u
+                for t in range(4):
+                    p = idx_s[t][0, at]
+                    n = idx_s[4 + t][0, at]
+                    dbuf[pl.ds(t * 32 + i * 8 + u, 1), :] = table[pl.ds(p, 1), :] - table[pl.ds(n, 1), :]
             return 0
 
-        lax.fori_loop(0, 128, body, 0, unroll=16)
-        for row in (row0, row0 + 1):
-            dt[q, :, row * 128:(row + 1) * 128] = dbuf[row * 128:(row + 1) * 128, :].T
+        lax.fori_loop(0, 4, body, 0)
+        cols = pl.ds(pl.multiple_of(row * 128, 128), 128)
+        dt[q, :, cols] = dbuf[...].T
+        if q:
+            remote(dt.at[1, :, cols], drecv.at[:, cols], ds, dr, xpeer).start()
+        return 0
 
     with jax.named_scope("ph_diff"):
-        for row0 in range(0, nrow, 2):
-            diff_rows(1, row0)
-            cols = pl.ds(row0 * 128, 256)
-            remote(dt.at[1, :, cols], drecv.at[:, cols], ds, dr, xpeer).start()
+        lax.fori_loop(0, nrow, lambda row, _: diff_row(1, row), 0)
 
     with jax.named_scope("ph_diff"):
-        for row0 in range(0, nrow // 2, 2):
-            diff_rows(0, row0)
+        lax.fori_loop(0, nrow // 2, lambda row, _: diff_row(0, row), 0)
 
     with jax.named_scope("ph_u3_wait"):
         rc_u3.wait_recv()
@@ -329,8 +341,7 @@
     rc_uf.start()
     ou_ref[...] = uall[:, pl.ds(pl.multiple_of(r * n_usr + c * uh, uh), uh)]
     with jax.named_scope("ph_diff"):
-        for row0 in range(nrow // 2, nrow, 2):
-            diff_rows(0, row0)
+        lax.fori_loop(nrow // 2, nrow, lambda row, _: diff_row(0, row), 0)
     with jax.named_scope("ph_uf_wait"):
         rc_uf.wait_recv()
     urow = jnp.dot(uall[...], sel[...], preferred_element_type=F32)
@@ -396,13 +407,13 @@
             vm((2 * dim, n_usr), F32), vm((2 * dim, n_usr), F32), vm((dim, n_usr), F32), vm((dim, n_usr), F32),
             vm((dim, 2 * n_usr), BF16), vm((2 * n_usr, nhome), BF16),
             vm((n_itm + 8, dim), F32),
-            vm((3, n_trip), jnp.int32), vm((128, 128), jnp.int32), vm((128, 128), jnp.int32),
-            pltpu.SMEM((128, 128), jnp.int32),
-            vm((nhome, dim), F32), vm((2, dim, nhome), F32), vm((dim, nhome), F32),
+            vm((3, n_trip), jnp.int32), vm((8, 1, 2 * nhome), jnp.int32),
+            *[pltpu.SMEM((1, 2 * nhome), jnp.int32)] * 8,
+            vm((128, dim), F32), vm((2, dim, nhome), F32), vm((dim, nhome), F32),
             vm((nhome // 128, 128), F32), vm((7, nhome // 128, 128), F32),
             dma((NSLOT,)), dma((3,)), dma((9,)), dma((9,)),
             dma(()), dma((n_itm // WIDE,)), dma(()), dma(()),
-            dma(()), dma(()), dma(()), dma(()), pltpu.SemaphoreType.REGULAR,
+            dma(()), dma(()), dma(()), dma(()), dma((8,)), pltpu.SemaphoreType.REGULAR,
         ]
         hbm_spec = pl.BlockSpec(memory_space=pltpu.HBM)
         vmem_spec = pl.BlockSpec(memory_space=pltpu.VMEM)

time: 47.8 us -> 47.3 us (0.990)
  Pallas kernels: 47.1 us -> 46.6 us
    pallas_call x1, Pallas kernels: 46.3 us -> 45.8 us  [local_fn(): pl.pallas_call(functools.partial(kernel, n_usr, n_itm, dim, n_trip), out_...]
where the time goes in v7:
time: 47.3 us; the launch traced here: 47.2 us
  Pallas kernels  46.6 us (99%)
  between operations  0.64 us (1%)
    pallas_call x1, Pallas kernels, local_fn(): pl.pallas_call(functools.partial(kernel, n_usr, n_itm, dim, n_trip), out_...  45.8 us

profile of v7, /device:TPU:0, one launch (start us, length us, event | category | flops | bytes accessed | tf_op | source)
XLA Modules:
  0.0 47.2 jit_solution(13164126194019805045)
XLA Ops:
  0.6 45.8 %gcn.1 = (bf16[32,256]{1,0:T(8,128)(2,1)S(1)}, bf16[32,8192]{1,0:T(8,128)(2,1)S(1)}, f32[32,128]{1,0:T(8,128)S(1)}) custom-call(s32[512,16384]{1,0:T(8,128)} %mask_ref.1, bf16[32,256]{1,0:T(8,128)(2,1)} %bitcast.8, bf16[32,8192]{1,0:T(8,128)(2,1)} %bitcast.6, s32[3,4096]{1,0:T(4,128)} %bitcast.7), custom_call_target="tpu_custom_call" | custom-call | tf_op jit(solution)/shard_map/gcn/pallas_call | solution.py:420
  46.4 0.8 %store.1 = (bf16[32,256]{1,0:T(8,128)(2,1)}, bf16[32,8192]{1,0:T(8,128)(2,1)}, f32[32,128]{1,0:T(8,128)}) custom-call(bf16[32,256]{1,0:T(8,128)(2,1)S(1)} %get-tuple-element.9.refs_0_, bf16[32,8192]{1,0:T(8,128)(2,1)S(1)} %get-tuple-element.10.refs_1_, f32[32,128]{1,0:T(8,128)S(1)} %get-tuple-element.11.refs_2_), custom_call_target="tpu_custom_call" | custom-call | tf_op jit(solution)/shard_map/store/pallas_call | solution.py:432

commit v8 on v7

--- a/solution.py
+++ b/solution.py
@@ -136,8 +136,6 @@
     invi[...] = lax.rsqrt(jnp.maximum(degi[...] + degi_r[...], 1.0))
     rc_i.wait_recv()
     rc_u.wait_recv()
-    for t in range(8):
-        cp_x[t].wait()
     with jax.named_scope("ph_du_wait"):
         rc_du.wait_recv()
     inv_row = lax.rsqrt(jnp.maximum(degu[...] + degu_r[...], 1.0))
@@ -323,6 +321,8 @@
             remote(dt.at[1, :, cols], drecv.at[:, cols], ds, dr, xpeer).start()
         return 0
 
+    for t in range(8):
+        cp_x[t].wait()
     with jax.named_scope("ph_diff"):
         lax.fori_loop(0, nrow, lambda row, _: diff_row(1, row), 0)
 

time: 47.3 us -> 47.3 us (level)
  no operation moved by 1% of the time
where the time goes in v8:
time: 47.3 us; the launch traced here: 47.2 us
  Pallas kernels  46.6 us (99%)
  between operations  0.64 us (1%)
    pallas_call x1, Pallas kernels, local_fn(): pl.pallas_call(functools.partial(kernel, n_usr, n_itm, dim, n_trip), out_...  45.8 us

profile of v8, /device:TPU:0, one launch (start us, length us, event | category | flops | bytes accessed | tf_op | source)
XLA Modules:
  0.0 47.2 jit_solution(4041900588186819071)
XLA Ops:
  0.6 45.8 %gcn.1 = (bf16[32,256]{1,0:T(8,128)(2,1)S(1)}, bf16[32,8192]{1,0:T(8,128)(2,1)S(1)}, f32[32,128]{1,0:T(8,128)S(1)}) custom-call(s32[512,16384]{1,0:T(8,128)} %mask_ref.1, bf16[32,256]{1,0:T(8,128)(2,1)} %bitcast.8, bf16[32,8192]{1,0:T(8,128)(2,1)} %bitcast.6, s32[3,4096]{1,0:T(4,128)} %bitcast.7), custom_call_target="tpu_custom_call" | custom-call | tf_op jit(solution)/shard_map/gcn/pallas_call | solution.py:420
  46.4 0.8 %store.1 = (bf16[32,256]{1,0:T(8,128)(2,1)}, bf16[32,8192]{1,0:T(8,128)(2,1)}, f32[32,128]{1,0:T(8,128)}) custom-call(bf16[32,256]{1,0:T(8,128)(2,1)S(1)} %get-tuple-element.9.refs_0_, bf16[32,8192]{1,0:T(8,128)(2,1)S(1)} %get-tuple-element.10.refs_1_, f32[32,128]{1,0:T(8,128)S(1)} %get-tuple-element.11.refs_2_), custom_call_target="tpu_custom_call" | custom-call | tf_op jit(solution)/shard_map/store/pallas_call | solution.py:432

commit v9 on v8

--- a/solution.py
+++ b/solution.py
@@ -82,7 +82,7 @@
             rowacc[rows, :] += s
             return acc + (m[0:8] + m[8:16])
 
-        acc = lax.fori_loop(0, n_usr // 16, rows_step, jnp.zeros((8, MC), F32), unroll=2)
+        acc = lax.fori_loop(0, n_usr // 16, rows_step, jnp.zeros((8, MC), F32), unroll=8)
         degi[pl.ds(j, 1), :] = jnp.sum(acc, axis=0, keepdims=True)
 
         @pl.when(j + NSLOT < n_itm // MC)

time: 47.3 us -> 47.2 us (level)
  no operation moved by 1% of the time
where the time goes in v9:
time: 47.2 us; the launch traced here: 47.1 us
  Pallas kernels  46.5 us (99%)
  between operations  0.64 us (1%)
    pallas_call x1, Pallas kernels, local_fn(): pl.pallas_call(functools.partial(kernel, n_usr, n_itm, dim, n_trip), out_...  45.7 us

profile of v9, /device:TPU:0, one launch (start us, length us, event | category | flops | bytes accessed | tf_op | source)
XLA Modules:
  0.0 47.1 jit_solution(12334212467040384728)
XLA Ops:
  0.6 45.7 %gcn.1 = (bf16[32,256]{1,0:T(8,128)(2,1)S(1)}, bf16[32,8192]{1,0:T(8,128)(2,1)S(1)}, f32[32,128]{1,0:T(8,128)S(1)}) custom-call(s32[512,16384]{1,0:T(8,128)} %mask_ref.1, bf16[32,256]{1,0:T(8,128)(2,1)} %bitcast.8, bf16[32,8192]{1,0:T(8,128)(2,1)} %bitcast.6, s32[3,4096]{1,0:T(4,128)} %bitcast.7), custom_call_target="tpu_custom_call" | custom-call | tf_op jit(solution)/shard_map/gcn/pallas_call | solution.py:420
  46.3 0.8 %store.1 = (bf16[32,256]{1,0:T(8,128)(2,1)}, bf16[32,8192]{1,0:T(8,128)(2,1)}, f32[32,128]{1,0:T(8,128)}) custom-call(bf16[32,256]{1,0:T(8,128)(2,1)S(1)} %get-tuple-element.9.refs_0_, bf16[32,8192]{1,0:T(8,128)(2,1)S(1)} %get-tuple-element.10.refs_1_, f32[32,128]{1,0:T(8,128)S(1)} %get-tuple-element.11.refs_2_), custom_call_target="tpu_custom_call" | custom-call | tf_op jit(solution)/shard_map/store/pallas_call | solution.py:432

commit v10 on v9

--- a/solution.py
+++ b/solution.py
@@ -32,7 +32,7 @@
            it0, it1, it2, ut0, i1p, i1r, i2p, i2r,
            up, up_r, u3p, u3_r, uall, sel, table,
            tri_v, idx_v, s0, s1, s2, s3, s4, s5, s6, s7, dbuf, dt, drecv, sbuf, srecv,
-           msem, lsem, ssem, rsem, cs1, cr1, cs2, cr2, ds, dr, bs, br, xsem, free_sem):
+           msem, lsem, ssem, rsem, cs1, cr1, cs2, cr2, ds, dr, bs, br, free_sem):
     idx_s = (s0, s1, s2, s3, s4, s5, s6, s7)
     e = lax.axis_index("emb")
     c = lax.axis_index("col")
@@ -127,7 +127,7 @@
                     idx_v[k * 4 + t, :, pl.ds((q * nrow + row) * 128, 32)] = loc[:, t * 32:(t + 1) * 32]
     cp_x = []
     for t in range(8):
-        cp_x.append(pltpu.make_async_copy(idx_v.at[t], idx_s[t], xsem.at[t]))
+        cp_x.append(pltpu.make_async_copy(idx_v.at[t], idx_s[t], msem.at[t]))
         cp_x[t].start()
     table[pl.ds(n_itm, 8), :] = jnp.zeros((8, dim), F32)
 
@@ -413,7 +413,7 @@
             vm((nhome // 128, 128), F32), vm((7, nhome // 128, 128), F32),
             dma((NSLOT,)), dma((3,)), dma((9,)), dma((9,)),
             dma(()), dma((n_itm // WIDE,)), dma(()), dma(()),
-            dma(()), dma(()), dma(()), dma(()), dma((8,)), pltpu.SemaphoreType.REGULAR,
+            dma(()), dma(()), dma(()), dma(()), pltpu.SemaphoreType.REGULAR,
         ]
         hbm_spec = pl.BlockSpec(memory_space=pltpu.HBM)
         vmem_spec = pl.BlockSpec(memory_space=pltpu.VMEM)

time: 47.2 us -> 47.2 us (level)
  no operation moved by 1% of the time
where the time goes in v10:
time: 47.2 us; the launch traced here: 47.1 us
  Pallas kernels  46.4 us (98%)
  between operations  0.64 us (1%)
    pallas_call x1, Pallas kernels, local_fn(): pl.pallas_call(functools.partial(kernel, n_usr, n_itm, dim, n_trip), out_...  45.6 us

profile of v10, /device:TPU:0, one launch (start us, length us, event | category | flops | bytes accessed | tf_op | source)
XLA Modules:
  0.0 47.1 jit_solution(10058410173573949641)
XLA Ops:
  0.6 45.6 %gcn.1 = (bf16[32,256]{1,0:T(8,128)(2,1)S(1)}, bf16[32,8192]{1,0:T(8,128)(2,1)S(1)}, f32[32,128]{1,0:T(8,128)S(1)}) custom-call(s32[512,16384]{1,0:T(8,128)} %mask_ref.1, bf16[32,256]{1,0:T(8,128)(2,1)} %bitcast.8, bf16[32,8192]{1,0:T(8,128)(2,1)} %bitcast.6, s32[3,4096]{1,0:T(4,128)} %bitcast.7), custom_call_target="tpu_custom_call" | custom-call | tf_op jit(solution)/shard_map/gcn/pallas_call | solution.py:420
  46.2 0.8 %store.1 = (bf16[32,256]{1,0:T(8,128)(2,1)}, bf16[32,8192]{1,0:T(8,128)(2,1)}, f32[32,128]{1,0:T(8,128)}) custom-call(bf16[32,256]{1,0:T(8,128)(2,1)S(1)} %get-tuple-element.9.refs_0_, bf16[32,8192]{1,0:T(8,128)(2,1)S(1)} %get-tuple-element.10.refs_1_, f32[32,128]{1,0:T(8,128)S(1)} %get-tuple-element.11.refs_2_), custom_call_target="tpu_custom_call" | custom-call | tf_op jit(solution)/shard_map/store/pallas_call | solution.py:432
